TPU v7x, 16 devices: a whole 2x2x2 slice. The times are simulated.
16 devices in a mesh: dp: 4 (over z, y), dap: 4 (over x, core).
Axes of the slice: x: 2, y: 2, z: 2, core: 2. Of those that a mesh axis runs over, the one named last changes fastest.
Arguments:
- z_pair: bfloat16 [4, 256, 256, 128], P('dp', 'dap')
- pair_mask: int32 [4, 256, 256], P('dp', 'dap')
- dz_out: bfloat16 [4, 256, 256, 128], P('dp', 'dap')
- ln_in: bfloat16 [2, 2, 128], replicated
- w_proj: bfloat16 [2, 128, 640], replicated
- b_proj: bfloat16 [2, 640], replicated
- ln_mid: bfloat16 [2, 2, 128], replicated
- w_out: bfloat16 [2, 128, 128], replicated
- b_out: bfloat16 [2, 128], replicated
Outputs:
- output 1: bfloat16 [4, 256, 256, 128], P('dp', 'dap')
- output 2: bfloat16 [4, 256, 256, 128], P('dp', 'dap')
- output 3: float32 [2, 2, 128], replicated
- output 4: float32 [2, 128, 640], replicated
- output 5: float32 [2, 640], replicated
- output 6: float32 [2, 2, 128], replicated
- output 7: float32 [2, 128, 128], replicated
- output 8: float32 [2, 128], replicated
All inputs are finite; a program needn't handle non-finite values.
Results may differ from a plain program's by a relative error of at most 0.01347.
Values are sent between devices in bfloat16 or wider.
A program may use at most 1 GiB of HBM per device.

v0:
```python
import jax
import jax.numpy as jnp
import functools
from jax import lax
from jax.sharding import PartitionSpec as P, NamedSharding

LN_EPS = 1e-5


def layer_norm(values, ln_gain, ln_bias):
    mean_val = jnp.mean(values, axis=-1, keepdims=True)
    centered = values - mean_val
    variance = jnp.mean(centered * centered, axis=-1, keepdims=True)
    return centered * lax.rsqrt(variance + LN_EPS) * ln_gain + ln_bias


def norm_bf16(values, ln_gain, ln_bias):
    return layer_norm(values, ln_gain, ln_bias).astype(jnp.bfloat16)


def split_gates(proj_all, mask_f, hidden):
    a_side = (jax.nn.sigmoid(proj_all[..., :hidden]) * proj_all[..., hidden:2 * hidden] * mask_f).astype(jnp.bfloat16)
    b_side = (jax.nn.sigmoid(proj_all[..., 2 * hidden:3 * hidden]) * proj_all[..., 3 * hidden:4 * hidden] * mask_f).astype(jnp.bfloat16)
    g_side = jax.nn.sigmoid(proj_all[..., 4 * hidden:])
    return a_side, b_side, g_side


def pre_forward(z_in, mask_f, ln_pair, w_proj, b_proj):
    hidden = (w_proj.shape[1] - w_proj.shape[0]) // 4
    z_hat, ln_pull = jax.vjp(norm_bf16, z_in.astype(jnp.float32), ln_pair[0], ln_pair[1])
    proj_all = jnp.einsum("pijc,ck->pijk", z_hat, w_proj, preferred_element_type=jnp.float32) + b_proj
    (a_side, b_side, g_side), gate_pull = jax.vjp(functools.partial(split_gates, mask_f=mask_f, hidden=hidden), proj_all)
    return a_side, b_side, g_side, (z_hat, ln_pull, gate_pull)


def post_forward(tri_x, g_side, z_in, ln_pair, w_out, b_out):
    x_hat, mid_pull = jax.vjp(norm_bf16, tri_x, ln_pair[0], ln_pair[1])
    update = jnp.einsum("pijh,hc->pijc", x_hat, w_out, preferred_element_type=jnp.float32) + b_out
    z_new = (z_in.astype(jnp.float32) + g_side * update).astype(jnp.bfloat16)
    return z_new, (x_hat, mid_pull, update)


def post_backward(dz_new, g_side, w_out, saved_parts):
    x_hat, mid_pull, update = saved_parts
    dz_f32 = dz_new.astype(jnp.float32)
    d_gate = dz_f32 * update
    d_update = dz_f32 * g_side
    d_b_out = jnp.sum(d_update, axis=(0, 1, 2))
    d_upd_bf = d_update.astype(jnp.bfloat16)
    d_w_out = jnp.einsum("pijh,pijc->hc", x_hat, d_upd_bf, preferred_element_type=jnp.float32)
    value_a6 = jnp.einsum("pijc,hc->pijh", d_upd_bf, w_out, preferred_element_type=jnp.float32).astype(jnp.bfloat16)
    d_tri, d_mid_gain, d_mid_bias = mid_pull(value_a6)
    return d_tri, d_gate, dz_f32, (jnp.stack([d_mid_gain, d_mid_bias]), d_w_out, d_b_out)


def pre_backward(d_a_side, d_b_side, d_gate, w_proj, saved_parts):
    z_hat, ln_pull, gate_pull = saved_parts
    (d_proj,) = gate_pull((d_a_side, d_b_side, d_gate))
    d_b_proj = jnp.sum(d_proj, axis=(0, 1, 2))
    d_proj_bf = d_proj.astype(jnp.bfloat16)
    d_w_proj = jnp.einsum("pijc,pijk->ck", z_hat, d_proj_bf, preferred_element_type=jnp.float32)
    d_zhat = jnp.einsum("pijk,ck->pijc", d_proj_bf, w_proj, preferred_element_type=jnp.float32).astype(jnp.bfloat16)
    dz_norm, d_in_gain, d_in_bias = ln_pull(d_zhat)
    return dz_norm, (jnp.stack([d_in_gain, d_in_bias]), d_w_proj, d_b_proj)


def collect_grads(pre_first, post_first, pre_second, post_second):
    return (jnp.stack([pre_first[0], pre_second[0]]), jnp.stack([pre_first[1], pre_second[1]]), jnp.stack([pre_first[2], pre_second[2]]), jnp.stack([post_first[0], post_second[0]]), jnp.stack([post_first[1], post_second[1]]), jnp.stack([post_first[2], post_second[2]]))


def solution(mesh):
    def local_step(z_pair, pair_mask, dz_out, ln_in, w_proj, b_proj, ln_mid, w_out, b_out):
        mask_f = pair_mask.astype(jnp.float32)[..., None]
        ln_in32 = ln_in.astype(jnp.float32)
        b_proj32 = b_proj.astype(jnp.float32)
        ln_mid32 = ln_mid.astype(jnp.float32)
        b_out32 = b_out.astype(jnp.float32)
        a_rows0, b_rows0, g_rows0, keep_pre0 = pre_forward(z_pair, mask_f, ln_in32[0], w_proj[0], b_proj32[0])
        b_full0 = lax.all_gather(b_rows0, "dap", axis=1, tiled=True)
        tri_x0 = jnp.einsum("pikc,pjkc->pijc", a_rows0, b_full0, preferred_element_type=jnp.float32)
        z_mid, keep_post0 = post_forward(tri_x0, g_rows0, z_pair, ln_mid32[0], w_out[0], b_out32[0])
        a_rows1, b_rows1, g_rows1, keep_pre1 = pre_forward(z_mid, mask_f, ln_in32[1], w_proj[1], b_proj32[1])
        a_cols1 = lax.all_to_all(a_rows1, "dap", 2, 1, tiled=True)
        b_full1 = lax.all_gather(b_rows1, "dap", axis=1, tiled=True)
        tri_x1 = jnp.einsum("pkic,pkjc->pijc", a_cols1, b_full1, preferred_element_type=jnp.float32)
        z_new, keep_post1 = post_forward(tri_x1, g_rows1, z_mid, ln_mid32[1], w_out[1], b_out32[1])
        d_tri1, d_gate1, d_res1, grads_post1 = post_backward(dz_out, g_rows1, w_out[1], keep_post1)
        d_trib1 = d_tri1.astype(jnp.bfloat16)
        d_acols1 = jnp.einsum("pijc,pkjc->pkic", d_trib1, b_full1, preferred_element_type=jnp.float32).astype(jnp.bfloat16)
        d_arows1 = lax.all_to_all(d_acols1, "dap", 1, 2, tiled=True)
        d_bpart1 = jnp.einsum("pkic,pijc->pkjc", a_cols1, d_trib1, preferred_element_type=jnp.float32).astype(jnp.bfloat16)
        d_brows1 = lax.psum_scatter(d_bpart1, "dap", scatter_dimension=1, tiled=True)
        dz_norm1, grads_pre1 = pre_backward(d_arows1, d_brows1, d_gate1, w_proj[1], keep_pre1)
        dz_mid = (d_res1 + dz_norm1).astype(jnp.bfloat16)
        d_tri0, d_gate0, d_res0, grads_post0 = post_backward(dz_mid, g_rows0, w_out[0], keep_post0)
        d_trib0 = d_tri0.astype(jnp.bfloat16)
        d_arows0 = jnp.einsum("pijc,pjkc->pikc", d_trib0, b_full0, preferred_element_type=jnp.float32).astype(jnp.bfloat16)
        d_bpart0 = jnp.einsum("pijc,pikc->pjkc", d_trib0, a_rows0, preferred_element_type=jnp.float32).astype(jnp.bfloat16)
        d_brows0 = lax.psum_scatter(d_bpart0, "dap", scatter_dimension=1, tiled=True)
        dz_norm0, grads_pre0 = pre_backward(d_arows0, d_brows0, d_gate0, w_proj[0], keep_pre0)
        dz_pair = (d_res0 + dz_norm0).astype(jnp.bfloat16)
        grads_all = lax.psum(collect_grads(grads_pre0, grads_post0, grads_pre1, grads_post1), ("dp", "dap"))
        return (z_new, dz_pair) + grads_all

    row_spec = P("dp", "dap")
    return jax.shard_map(local_step, mesh=mesh, in_specs=(row_spec, row_spec, row_spec, P(), P(), P(), P(), P(), P()), out_specs=(row_spec, row_spec, P(), P(), P(), P(), P(), P()), check_vma=False)
```

profile of v0, /device:TPU:0, one launch (start us, length us, event | category | flops | bytes accessed | tf_op | source)
XLA Modules:
  0.0 1112.4 jit_solution(3719928293933977283)
XLA Ops:
  20.2 15.3 %add_bitcast_fusion.1 = f32[1,64,256,640]{3,2,1,0:T(8,128)} fusion(f32[640]{0:T(1024)S(1)} %get-tuple-element.19, bf16[1,64,256,128]{3,2,1,0:T(8,128)(2,1)S(1)} %copy-done.1, f32[128]{0:T(128)S(1)} %get-tuple-element.68, f32[128]{0:T(128)S(1)} %get-tuple-element.69, f32[64,256]{1,0:T(8,128)S(1)} %fusion.159, f32[64,256]{1,0:T(8,128)S(1)} %broadcast_multiply_fusion.3, ...), kind=kOutput, calls=%fused_computation.3 | convolution fusion | flops 2707423232 | bytes 46437376 | tf_op jit(solution)/shard_map/pijc,ck->pijk/dot_general | solution.py:31
  35.6 15.4 %fusion.104 = (bf16[1,64,256,128]{3,2,0,1:T(8,128)(2,1)}, bf16[64,256,128]{2,1,0:T(8,128)(2,1)}) fusion(f32[1,64,256,640]{3,2,1,0:T(8,128)} %add_bitcast_fusion.1, f32[64,256]{1,0:T(8,128)S(1)} %convert_bitcast_fusion.9), kind=kLoop, calls=%fused_computation.171 | loop fusion | flops 25165824 | bytes 42008576 | tf_op jit(solution)/shard_map/jvp()/convert_element_type | solution.py:23
  58.6 100.4 %all-gather.3.cloned.1.call-done = bf16[1,256,256,128]{3,2,0,1:T(8,128)(2,1)} async-done(((bf16[1,64,256,128]{3,2,0,1:T(8,128)(2,1)}), bf16[1,256,256,128]{3,2,0,1:T(8,128)(2,1)}) %all-gather.3.cloned.1.call-update) | async-done | bytes 16777232 | tf_op jit(solution)/shard_map/all_gather | solution.py:79
  159.1 23.4 %copy.119 = bf16[1,256,256,128]{2,1,3,0:T(8,128)(2,1)} copy(bf16[1,256,256,128]{3,2,0,1:T(8,128)(2,1)} %all-gather.3.cloned.1.call-done) | data formatting | bytes 33554432 | tf_op jit(solution)/shard_map/all_gather | solution.py:79
  182.5 12.7 %bitcast_reduce_fusion.1 = (f32[64,256]{1,0:T(8,128)S(1)}, f32[128,256,64]{1,2,0:T(8,128)}) fusion(bf16[64,256,128]{1,0,2:T(8,128)(2,1)} %copy.120, bf16[1,256,256,128]{2,1,3,0:T(8,128)(2,1)} %copy.119), kind=kOutput, calls=%fused_computation.147 | convolution fusion | flops 1075822592 | bytes 29425664 | tf_op jit(solution)/shard_map/pikc,pjkc->pijc/dot_general | solution.py:80
  202.7 12.8 %convert_reduce_fusion.4 = (f32[64,256]{1,0:T(8,128)S(1)}, bf16[1,64,256,128]{3,2,1,0:T(8,128)(2,1)S(1)}, f32[64,256,128]{2,1,0:T(8,128)}) fusion(f32[128]{0:T(128)S(1)} %get-tuple-element.71, f32[1,64,256,640]{3,2,1,0:T(8,128)} %add_bitcast_fusion.1, bf16[1,64,256,128]{3,2,1,0:T(8,128)(2,1)S(1)} %copy-done.2, bf16[2,128,128]{2,1,0:T(8,128)(2,1)S(1)} %copy-done.58, ...), kind=kOutput, calls=%fused_computation.56 | convolution fusion | flops 557826048 | bytes 29458944 | tf_op jit(solution)/shard_map/pijh,hc->pijc/dot_general | solution.py:38
  220.3 15.3 %add_bitcast_fusion = f32[1,64,256,640]{3,2,1,0:T(8,128)} fusion(f32[640]{0:T(1024)S(1)} %get-tuple-element.18, bf16[1,64,256,128]{3,2,1,0:T(8,128)(2,1)S(1)} %get-tuple-element.29, f32[128]{0:T(128)S(1)} %get-tuple-element.67, f32[128]{0:T(128)S(1)} %get-tuple-element.66, f32[64,256]{1,0:T(8,128)S(1)} %fusion.161, ...), kind=kOutput, calls=%fused_computation.2 | convolution fusion | flops 2707423232 | bytes 46437376 | tf_op jit(solution)/shard_map/pijc,ck->pijk/dot_general | solution.py:31
  235.7 15.6 %fusion.107 = (bf16[1,64,256,128]{3,2,0,1:T(8,128)(2,1)}, bf16[1,64,256,128]{3,2,1,0:T(8,128)(2,1)}) fusion(f32[1,64,256,640]{3,2,1,0:T(8,128)} %add_bitcast_fusion, f32[64,256]{1,0:T(8,128)S(1)} %convert_bitcast_fusion.9), kind=kLoop, calls=%fused_computation.174 | loop fusion | flops 25165824 | bytes 42008576 | tf_op jit(solution)/shard_map/jvp()/convert_element_type | solution.py:23
  278.9 77.4 %all-to-all-done = bf16[1,64,256,128]{3,1,0,2:T(8,128)(2,1)} async-done(((bf16[1,64,256,128]{3,1,0,2:T(8,128)(2,1)}), bf16[1,64,256,128]{3,1,0,2:T(8,128)(2,1)}, u32[]{:S(2)}, u32[]{:S(2)}) %all-to-all-start) | async-done | bytes 4194336 | tf_op jit(solution)/shard_map/all_to_all | solution.py:83
  371.5 29.9 %all-gather.5.cloned.1.call-done = bf16[1,256,256,128]{3,2,0,1:T(8,128)(2,1)} async-done(((bf16[1,64,256,128]{3,2,0,1:T(8,128)(2,1)}), bf16[1,256,256,128]{3,2,0,1:T(8,128)(2,1)}) %all-gather.5.cloned.1.call-update) | async-done | bytes 16777232 | tf_op jit(solution)/shard_map/all_gather | solution.py:84
  401.5 22.4 %copy.125 = bf16[1,256,256,128]{2,1,3,0:T(8,128)(2,1)} copy(bf16[1,256,256,128]{3,2,0,1:T(8,128)(2,1)} %all-gather.5.cloned.1.call-done) | data formatting | bytes 33554432 | tf_op jit(solution)/shard_map/all_gather | solution.py:84
  460.3 24.3 %copy.133 = bf16[128,256,256]{0,1,2:T(8,128)(2,1)} copy(bf16[128,256,256]{2,1,0:T(8,128)(2,1)} %fusion.183) | data formatting | bytes 33554432 | tf_op jit(solution)/shard_map/pkic,pijc->pkjc/dot_general | solution.py:91
  504.1 94.1 %all_to_all.24 = bf16[1,256,64,128]{3,2,0,1:T(8,128)(2,1)S(1)} all-to-all(bf16[1,256,64,128]{3,2,0,1:T(8,128)(2,1)} %copy.134), channel_id=1, replica_groups=mesh['dp'=4,'dap'=4] {'dap'}, dimensions={1} | all-to-all | bytes 8388608 | tf_op jit(solution)/shard_map/all_to_all | solution.py:90
  603.3 43.9 %reduce-scatter.3.cloned.1.call-done = bf16[1,64,256,128]{3,2,1,0:T(8,128)(2,1)} async-done(((bf16[1,256,256,128]{3,2,1,0:T(8,128)(2,1)}), bf16[1,64,256,128]{3,2,1,0:T(8,128)(2,1)}) %reduce-scatter.3.cloned.1.call-update) | async-done | bytes 4194320 | tf_op jit(solution)/shard_map/reduce_scatter | solution.py:92
  647.2 37.7 %fusion.60 = (f32[1,64,256,128]{3,2,1,0:T(8,128)}, bf16[1,64,256,128]{3,2,1,0:T(8,128)(2,1)}, f32[128]{0:T(128)S(1)}, f32[1,64,256,128]{3,2,1,0:T(8,128)}, f32[1...) fusion(bf16[1,64,256,128]{3,2,1,0:T(8,128)(2,1)} %param.11, ...), kind=kOutput, calls=%fused_computation.100 | convolution fusion | flops 608173952 | bytes 113345536 | tf_op jit(solution)/shard_map/pijh,hc->pijc/dot_general | solution.py:38
  684.9 24.2 %fusion.8 = (f32[640]{0:T(1024)S(1)}, bf16[1,64,256,640]{3,2,1,0:T(8,128)(2,1)}) fusion(f32[1,64,256,128]{3,2,1,0:T(8,128)} %get-tuple-element.55, f32[1,64,256,128]{3,2,1,0:T(8,128)} %get-tuple-element.54, f32[1,64,256,128]{3,2,1,0:T(8,128)} %get-tuple-element.56, f32[1,64,256,128]{3,2,1,0:T(8,128)} %get-tuple-element.57, ...), kind=kLoop, calls=%fused_computation.12 | loop fusion | flops 62913920 | bytes 62917120 | tf_op jit(solution)/shard_map/reduce_sum | solution.py:59
  719.7 13.0 %fusion.42 = (f32[128]{0:T(128)}, f32[64,256]{1,0:T(8,128)S(1)}) fusion(bf16[1,64,256,128]{3,2,1,0:T(8,128)(2,1)S(1)} %copy-done.11, bf16[64,256,128]{2,1,0:T(8,128)(2,1)S(1)} %get-tuple-element.78, f32[64,256]{1,0:T(8,128)S(1)} %copy-done.30, f32[64,256]{1,0:T(8,128)S(1)} %copy-done.28, f32[64,256]{1,0:T(8,128)S(1)} %multiply_multiply_fusion.2, ...), kind=kLoop, calls=%fused_computation.82 | loop fusion | flops 25149312 | bytes 8651776 | tf_op jit(solution)/shard_map/transpose(jvp())/reduce_sum | solution.py:14
  787.7 24.3 %copy.140 = bf16[128,256,256]{0,1,2:T(8,128)(2,1)} copy(bf16[128,256,256]{2,1,0:T(8,128)(2,1)} %fusion.184) | data formatting | bytes 33554432 | tf_op jit(solution)/shard_map/pijc,pikc->pjkc/dot_general | solution.py:98
  859.3 13.6 %fusion.135 = f32[1,128,640]{2,1,0:T(8,128)S(1)} fusion(bf16[1,64,256,640]{3,2,1,0:T(8,128)(2,1)} %get-tuple-element.52, bf16[1,64,256,128]{3,2,1,0:T(8,128)(2,1)S(1)} %copy-done.12, f32[128]{0:T(128)S(1)} %copy-done.51, f32[128]{0:T(128)S(1)} %copy-done.45, f32[64,256]{1,0:T(8,128)S(1)} %copy-done.30, f32[64,256]{1,0:T(8,128)S(1)} %copy-done.28), kind=kOutput, calls=%fused_computation.193 | convolution fusion | flops 2696937472 | bytes 25625600 | tf_op jit(solution)/shard_map/pijc,pijk->ck/dot_general | solution.py:61
  873.0 59.7 %reduce-scatter.5.cloned.1.call-done = bf16[1,64,256,128]{3,2,1,0:T(8,128)(2,1)} async-done(((bf16[1,256,256,128]{3,2,1,0:T(8,128)(2,1)}), bf16[1,64,256,128]{3,2,1,0:T(8,128)(2,1)}) %reduce-scatter.5.cloned.1.call-update) | async-done | bytes 4194320 | tf_op jit(solution)/shard_map/reduce_scatter | solution.py:99
  932.7 35.9 %fusion.93 = (f32[1,64,256,128]{3,2,1,0:T(8,128)}, f32[1,64,256,128]{3,2,1,0:T(8,128)}, f32[1,64,256,128]{3,2,1,0:T(8,128)}, f32[1,64,256,128]{3,2,1,0:T(8,128)}, f32[1,64,256,128]{3,2,1,0:T(8,128)}) fusion(bf16[1,64,256,128]{3,2,1,0:T(8,128)(2,1)} %reduce-scatter.5.cloned.1.call-done, f32[64,256]{1,0:T(8,128)S(1)} %convert_bitcast_fusion.9, ...), kind=kLoop, calls=%fused_computation.149 | loop fusion | flops 60817408 | bytes 104923648 | tf_op jit(solution)/shard_map/transpose(jvp())/mul | solution.py:23
  968.7 17.3 %fusion.10 = (f32[640]{0:T(1024)S(1)}, bf16[1,64,256,640]{3,2,1,0:T(8,128)(2,1)S(1)}) fusion(f32[1,64,256,128]{3,2,1,0:T(8,128)} %get-tuple-element.41, f32[1,64,256,128]{3,2,1,0:T(8,128)} %get-tuple-element.42, f32[1,64,256,128]{3,2,1,0:T(8,128)} %get-tuple-element.35, f32[1,64,256,128]{3,2,1,0:T(8,128)} %get-tuple-element.34, ...), kind=kLoop, calls=%fused_computation.14 | loop fusion | flops 62913920 | bytes 62917120 | tf_op jit(solution)/shard_map/reduce_sum | solution.py:59
  1039.8 32.3 %all-reduce.10 = (f32[2,2,128]{2,1,0:T(2,128)}, f32[2,640]{1,0:T(2,128)}, f32[2,2,128]{2,1,0:T(2,128)}, f32[2,128]{1,0:T(2,128)}) all-reduce(f32[2,2,128]{2,1,0:T(2,128)S(1)} %pad_maximum_fusion.3, f32[2,640]{1,0:T(2,128)S(1)} %pad_maximum_fusion.2, ...), channel_id=1, replica_groups=mesh['dp'=4,'dap'=4] {'dp','dap'}, use_global_device_ids=true, to_apply=%region_22.0 | all-reduce | flops 2560 | bytes 20480 | tf_op jit(solution)/shard_map/psum | solution.py:102
  1072.1 30.0 %all-reduce.14.cloned.1.call-done = (f32[2,128,640]{2,1,0:T(8,128)}, f32[2,128,128]{2,1,0:T(8,128)}) async-done(((f32[2,128,640]{2,1,0:T(8,128)}, f32[2,128,128]{2,1,0:T(8,128)}), (f32[2,128,640]{2,1,0:T(8,128)}, f32[2,128,128]{2,1,0:T(8,128)})) %all-reduce.14.cloned.1.call-update) | async-done | bytes 786448 | tf_op jit(solution)/shard_map/psum | solution.py:102
  (213 shorter events, 306.3 us)
Async XLA Ops:
  7.2 151.9 %all-gather.3.cloned.1.call-start = ((), (), s32[]{:S(2)}) async-start(), calls=%async_computation.4 | async-start | bytes 20971520 | tf_op jit(solution)/shard_map/all_gather | solution.py:79
  8.1 27.4 %copy-start.42 = (f32[128]{0:T(128)}, f32[128]{0:T(128)S(1)}, u32[]{:S(2)}) copy-start(f32[128]{0:T(128)S(1)} %get-tuple-element.69) | copy-start | bytes 1540
  8.1 27.4 %copy-start.48 = (f32[128]{0:T(128)}, f32[128]{0:T(128)S(1)}, u32[]{:S(2)}) copy-start(f32[128]{0:T(128)S(1)} %get-tuple-element.68) | copy-start | bytes 1540
  8.1 212.2 %copy-start.44 = (f32[128]{0:T(128)}, f32[128]{0:T(128)S(1)}, u32[]{:S(2)}) copy-start(f32[128]{0:T(128)S(1)} %get-tuple-element.66) | copy-start | bytes 1540
  8.1 212.2 %copy-start.50 = (f32[128]{0:T(128)}, f32[128]{0:T(128)S(1)}, u32[]{:S(2)}) copy-start(f32[128]{0:T(128)S(1)} %get-tuple-element.67) | copy-start | bytes 1540
  51.0 350.5 %all-gather.5.cloned.1.call-start = ((), (), s32[]{:S(2)}) async-start(), calls=%async_computation.5 | async-start | bytes 20971520 | tf_op jit(solution)/shard_map/all_gather | solution.py:84
  58.6 144.0 %copy-start.52 = (f32[128]{0:T(128)}, f32[128]{0:T(128)S(1)}, u32[]{:S(2)}) copy-start(f32[128]{0:T(128)S(1)} %get-tuple-element.71) | copy-start | bytes 1540
  58.6 141.1 %copy-start.46 = (f32[128]{0:T(128)}, f32[128]{0:T(128)S(1)}, u32[]{:S(2)}) copy-start(f32[128]{0:T(128)S(1)} %get-tuple-element.65) | copy-start | bytes 1540
  258.2 98.1 %all-to-all-start = ((bf16[1,64,256,128]{3,1,0,2:T(8,128)(2,1)}), bf16[1,64,256,128]{3,1,0,2:T(8,128)(2,1)}, u32[]{:S(2)}, u32[]{:S(2)}) async-start(bf16[1,64,256,128]{3,1,0,2:T(8,128)(2,1)} %copy.126), calls=%async_computation | async-start | bytes 8388608 | tf_op jit(solution)/shard_map/all_to_all | solution.py:83
  263.1 384.1 %reduce-scatter.3.cloned.1.call-start = ((), (), s32[]{:S(2)}) async-start(), calls=%async_computation.6 | async-start | bytes 20971520 | tf_op jit(solution)/shard_map/reduce_scatter | solution.py:92
  484.6 448.1 %reduce-scatter.5.cloned.1.call-start = ((), (), s32[]{:S(2)}) async-start(), calls=%async_computation.7 | async-start | bytes 20971520 | tf_op jit(solution)/shard_map/reduce_scatter | solution.py:99
  599.2 48.0 %copy-start.57 = (f32[128]{0:T(128)S(1)}, f32[128]{0:T(128)}, u32[]{:S(2)}) copy-start(f32[128]{0:T(128)} %get-tuple-element.70) | copy-start | bytes 1540
  684.9 24.3 %copy-start.11 = (bf16[1,64,256,128]{3,2,1,0:T(8,128)(2,1)S(1)}, bf16[1,64,256,128]{3,2,1,0:T(8,128)(2,1)}, u32[]{:S(2)}) copy-start(bf16[1,64,256,128]{3,2,1,0:T(8,128)(2,1)} %copy-done.10) | copy-start | bytes 12582916
  684.9 24.3 %copy-start.28 = (f32[64,256]{1,0:T(8,128)S(1)}, f32[64,256]{1,0:T(8,128)}, u32[]{:S(2)}) copy-start(f32[64,256]{1,0:T(8,128)} %copy-done.27) | copy-start | bytes 196612
  684.9 24.3 %copy-start.40 = (bf16[2,128,640]{2,1,0:T(8,128)(2,1)S(1)}, bf16[2,128,640]{2,1,0:T(8,128)(2,1)}, u32[]{:S(2)}) copy-start(bf16[2,128,640]{2,1,0:T(8,128)(2,1)} %param.13) | copy-start | bytes 983044
  684.9 24.3 %copy-start.45 = (f32[128]{0:T(128)S(1)}, f32[128]{0:T(128)}, u32[]{:S(2)}) copy-start(f32[128]{0:T(128)} %copy-done.44) | copy-start | bytes 1540
  719.6 24.9 %copy-start.15 = (bf16[64,256,128]{2,1,0:T(8,128)(2,1)}, bf16[64,256,128]{2,1,0:T(8,128)(2,1)S(1)}, u32[]{:S(2)}) copy-start(bf16[64,256,128]{2,1,0:T(8,128)(2,1)S(1)} %get-tuple-element.78) | copy-start | bytes 12582916
  812.0 290.1 %all-reduce.14.cloned.1.call-start = ((), (), s32[]{:S(2)}) async-start(), calls=%async_computation.8 | async-start | bytes 1572864 | tf_op jit(solution)/shard_map/psum | solution.py:102
  859.3 73.4 %copy-start.53 = (f32[128]{0:T(128)S(1)}, f32[128]{0:T(128)}, u32[]{:S(2)}) copy-start(f32[128]{0:T(128)} %copy-done.52) | copy-start | bytes 1540
  968.6 24.4 %copy-start.3 = (bf16[1,64,256,128]{3,2,1,0:T(8,128)(2,1)S(1)}, bf16[1,64,256,128]{3,2,1,0:T(8,128)(2,1)}, u32[]{:S(2)}) copy-start(bf16[1,64,256,128]{3,2,1,0:T(8,128)(2,1)} %param.9) | copy-start | bytes 12582916
  968.6 24.4 %copy-start.24 = (f32[64,256]{1,0:T(8,128)S(1)}, f32[64,256]{1,0:T(8,128)}, u32[]{:S(2)}) copy-start(f32[64,256]{1,0:T(8,128)} %copy-done.23) | copy-start | bytes 196612
  968.6 24.4 %copy-start.26 = (f32[64,256]{1,0:T(8,128)S(1)}, f32[64,256]{1,0:T(8,128)}, u32[]{:S(2)}) copy-start(f32[64,256]{1,0:T(8,128)} %copy-done.25) | copy-start | bytes 196612
  968.6 24.4 %copy-start.43 = (f32[128]{0:T(128)S(1)}, f32[128]{0:T(128)}, u32[]{:S(2)}) copy-start(f32[128]{0:T(128)} %copy-done.42) | copy-start | bytes 1540
  968.7 24.3 %copy-start.49 = (f32[128]{0:T(128)S(1)}, f32[128]{0:T(128)}, u32[]{:S(2)}) copy-start(f32[128]{0:T(128)} %copy-done.48) | copy-start | bytes 1540
  (44 other events, 445.1 us)
Sparse Core Ops, SparseCore 0:
  51.1 107.9 all-gather.2
  251.4 150.0 all-gather.4
  484.7 162.4 reduce-scatter.2
  812.1 120.5 reduce-scatter.4
  1035.5 66.5 all-reduce.13
where the time goes:
time: 1120 us; the launch traced here: 1110 us
  waiting for transfers between devices  341 us (30%)
  other arithmetic  226 us (20%)
  matrix products  224 us (20%)
  local copies, waits for them, and re-layouts  175 us (16%)
  blocking collectives  126 us (11%)
  between operations  15 us (1%)
    all_gather x1, waiting for transfers between devices, local_step(): b_full0 = lax.all_gather(b_rows0, 'dap', axis=1, tiled=True)  100 us
    all_to_all x1, blocking collectives, local_step(): d_arows1 = lax.all_to_all(d_acols1, 'dap', 1, 2, tiled=True)  94.1 us
    all_to_all x1, waiting for transfers between devices, local_step(): a_cols1 = lax.all_to_all(a_rows1, 'dap', 2, 1, tiled=True)  77.4 us
    reduce_sum x10, other arithmetic, layer_norm(): return centered * lax.rsqrt(variance + LN_EPS) * ln_gain + ln_bias  59.7 us
    reduce_scatter x1, waiting for transfers between devices, local_step(): lax.psum_scatter(d_bpart0, 'dap', scatter_dimension=1, tiled=True)  59.7 us
    dot_general x2, matrix products, post_forward(): jnp.einsum('pijh,hc->pijc', x_hat, w_out, preferred_element_type=jnp.floa...  50.5 us
    reduce_scatter x1, waiting for transfers between devices, local_step(): lax.psum_scatter(d_bpart1, 'dap', scatter_dimension=1, tiled=True)  43.9 us
    reduce_sum x2, other arithmetic, pre_backward(): d_b_proj = jnp.sum(d_proj, axis=(0, 1, 2))  41.6 us
  transfers between devices with their start and end apart: 6, of which 6 were waited for; matrix products, arithmetic and copies ran while one was open for 12% of the time, Pallas kernels for 0%

commit v1 on v0

v1 whole, which is shorter than its diff:
```python
import functools
import jax
import jax.numpy as jnp
from jax import lax
from jax.experimental import pallas as pl
from jax.experimental.pallas import tpu as pltpu
from jax.sharding import PartitionSpec as P

LN_EPS = 1e-5
RB = 16
SP = 17
UN = 4
F32 = jnp.float32
BF16 = jnp.bfloat16
C = 128
N = 256
QUAD = [[0, 2, 1, 3]]
SWAP_X = [(0, 2), (2, 0), (1, 3), (3, 1)]


def dot(a, b):
    return lax.dot_general(a, b, (((1,), (0,)), ((), ())), preferred_element_type=F32)


def dot_t(a, b):
    return dot(a, jnp.transpose(b))


def sig(v):
    return 0.5 * jnp.tanh(0.5 * v) + 0.5


def norm(v):
    mu = jnp.mean(v, axis=0, keepdims=True)
    vc = v - mu
    rstd = lax.rsqrt(jnp.mean(vc * vc, axis=0, keepdims=True) + LN_EPS)
    return vc * rstd, rstd


def norm_bwd(d_hat, vn, rstd, gain):
    dn = d_hat * gain
    m1 = jnp.mean(dn, axis=0, keepdims=True)
    m2 = jnp.mean(dn * vn, axis=0, keepdims=True)
    return rstd * (dn - m1 - vn * m2)


def perm_cols(t):
    return jnp.concatenate([t[0:64], t[128:192], t[64:128], t[192:256]], axis=0)


def load_t(ref, r):
    return jnp.transpose(perm_cols(ref[r])).astype(F32)


def store_t(ref, r, val):
    t = perm_cols(jnp.transpose(val)).astype(BF16)
    ref[r] = t


def put_row(scr, r, val):
    for h in range(2):
        scr[h, pl.ds(r, C, stride=SP), :] = val[:, h * 128:(h + 1) * 128]


def get_row(scr, r):
    return jnp.concatenate([scr[h, pl.ds(r, C, stride=SP), :] for h in range(2)], axis=1)


def pack(scr, out_ref):
    def body(i, _):
        c0 = i * 8
        for k in range(8):
            for h in range(2):
                out_ref[c0 + k, :, h * 128:(h + 1) * 128] = scr[h, pl.ds((c0 + k) * SP, RB), :].astype(out_ref.dtype)
        return 0
    lax.fori_loop(0, C // 8, body, 0)


def unpack(in_ref, scr):
    def body(i, _):
        c0 = i * 8
        for k in range(8):
            for h in range(2):
                scr[h, pl.ds((c0 + k) * SP, RB), :] = in_ref[c0 + k, :, h * 128:(h + 1) * 128].astype(F32)
        return 0
    lax.fori_loop(0, C // 8, body, 0)


def gates(zh, m, wt, bp, scr_a, scr_b, r):
    pa = dot(wt[0:256, :], zh)
    put_row(scr_a, r, sig(pa[0:128] + bp[0]) * (pa[128:256] + bp[1]) * m)
    pb = dot(wt[256:512, :], zh)
    put_row(scr_b, r, sig(pb[0:128] + bp[2]) * (pb[128:256] + bp[3]) * m)


CHUNKS = ((0, 640, (0, 1, 2, 3)), (640, 512, (0, 2, 3, 1)), (1152, 512, (0, 3, 1, 2)))
GROWS = 1664


def coords():
    return lax.axis_index("dp"), lax.axis_index("dap")


def partner(k):
    dp, dap = coords()
    if k < 2:
        bit = lax.rem(dap // (1 << k), 2)
        return bit, (dp, dap + (1 << k) * (1 - 2 * bit))
    bit = lax.rem(dp // (1 << (k - 2)), 2)
    return bit, (dp + (1 << (k - 2)) * (1 - 2 * bit), dap)


def greet(keys):
    barrier = pltpu.get_barrier_semaphore()
    for k in keys:
        pl.semaphore_signal(barrier, inc=1, device_id=partner(k)[1], device_id_type=pl.DeviceIdType.MESH)
    pl.semaphore_wait(barrier, len(keys))


def remote(src, dst, send, recv, k):
    return pltpu.make_async_remote_copy(src_ref=src, dst_ref=dst, send_sem=send, recv_sem=recv, device_id=partner(k)[1], device_id_type=pl.DeviceIdType.MESH)


def rb(i):
    return lax.rem(i + 4 * partner(1)[0], 8)


def first4(i):
    return lax.min(i, 3)


def pair_parts(step, st, out, split):
    bit = partner(0)[0]
    slot = lax.rem(step, 2)
    dst = out.at[:, pl.ds(pl.multiple_of(bit * 128 + rb(step) * RB, RB), RB), :]
    mine = theirs = st.at[slot]
    if split:
        mine = st.at[slot, :, :, pl.ds(pl.multiple_of(bit * 128, 128), 128)]
        theirs = st.at[slot, :, :, pl.ds(pl.multiple_of((1 - bit) * 128, 128), 128)]
    return slot, dst, mine, theirs


def pair_here(step, st, out, sems, split):
    slot, dst, mine, _ = pair_parts(step, st, out, split)
    return pltpu.make_async_copy(mine, dst, sems[0].at[slot])


def pair_there(step, st, out, sems, split):
    slot, dst, _, theirs = pair_parts(step, st, out, split)
    return remote(theirs, dst, sems[1].at[slot], sems[2].at[step], 0)


def ship(step, items):
    @pl.when(step >= 2)
    def _():
        for _, *it in items:
            pair_here(step - 2, *it).wait()
            pair_there(step - 2, *it).wait_send()
    for scr, *it in items:
        pack(scr, it[0].at[lax.rem(step, 2)])
        pair_here(step, *it).start()
        pair_there(step, *it).start()

    @pl.when(step == 7)
    def _():
        for _, *it in items:
            for k in (6, 7):
                pair_here(k, *it).wait()
                pair_there(k, *it).wait_send()
            for k in range(8):
                pair_there(k, *it).wait_recv()


def ship_scratch():
    return [pltpu.VMEM((2, C, RB, N), BF16), pltpu.SemaphoreType.DMA((2,)), pltpu.SemaphoreType.DMA((2,)), pltpu.SemaphoreType.DMA((8,))]


def pre_kernel(z_ref, m_ref, ln_ref, wt_ref, bp_ref, a_ref, zh_ref, zt_ref, mall_ref, af_ref, bf_ref,
               scr_a, scr_b, mbuf, zbuf, zloc, zsend, zrecv, msem, st_a, la, sa, ra, st_b, lb, sb, rb_):
    step = pl.program_id(0)
    xb = partner(1)[0]

    def z_here(q):
        return pltpu.make_async_copy(z_ref.at[pl.ds(q * RB, RB)], zbuf.at[pl.ds(q * RB, RB)], zloc.at[q])

    def z_there(q):
        return remote(z_ref.at[pl.ds(q * RB, RB)], zbuf.at[pl.ds(64 + q * RB, RB)], zsend.at[q], zrecv.at[q], 1)

    m_dst = mbuf.at[pl.ds(pl.multiple_of(xb * 64, 64), 64), :]

    def m_there():
        return remote(m_ref, m_dst, msem.at[1], msem.at[2], 1)

    @pl.when(step == 0)
    def _():
        for q in range(4):
            z_here(q).start()
        greet((0, 1))
        m_here = pltpu.make_async_copy(m_ref, m_dst, msem.at[0])
        m_here.start()
        m_there().start()
        for q in range(4):
            z_there(q).start()
        m_here.wait()
    for q in range(4):
        @pl.when(step == q)
        def _():
            z_here(q).wait()

        @pl.when(step == 4 + q)
        def _():
            if q == 0:
                m_there().wait()
            z_there(q).wait()

    def row(r, _):
        zt = load_t(zbuf, step * RB + r)
        zt_ref[r] = zt.astype(BF16)
        zn, _ = norm(zt)
        zh = (zn * ln_ref[0] + ln_ref[1]).astype(BF16)
        zh_ref[r] = zh
        gates(zh, mbuf[pl.ds(rb(step) * RB + r, 1), :], wt_ref, bp_ref, scr_a, scr_b, r)
        return 0
    lax.fori_loop(0, RB, row, 0, unroll=UN)
    ship(step, [(scr_a, st_a, af_ref, (la, sa, ra), False), (scr_b, st_b, bf_ref, (lb, sb, rb_), False)])
    a_ref[...] = st_a[lax.rem(step, 2)]

    @pl.when(step == 7)
    def _():
        mall_ref[...] = mbuf[...]


def mid_kernel(x_ref, zh_ref, zt_ref, m_ref, lnm_ref, wot_ref, bo_ref, wgt_ref, bg_ref, ln_ref, wt_ref, bp_ref,
               zm_ref, zh1_ref, ao_ref, bo1_ref, ac_ref, bf_ref, scr_x, scr_a, scr_b, st_a, la, sa, ra, st_b, lb, sb, rb_):
    step = pl.program_id(0)

    @pl.when(step == 0)
    def _():
        greet((0,))
    unpack(x_ref, scr_x)

    def row(r, _):
        xn, _ = norm(get_row(scr_x, r))
        xh = (xn * lnm_ref[0] + lnm_ref[1]).astype(BF16)
        u = dot(wot_ref[...], xh) + bo_ref[...]
        g = sig(dot(wgt_ref[...], zh_ref[r]) + bg_ref[...])
        zm = (zt_ref[r].astype(F32) + g * u).astype(BF16)
        zm_ref[r] = zm
        zn, _ = norm(zm.astype(F32))
        zh = (zn * ln_ref[0] + ln_ref[1]).astype(BF16)
        zh1_ref[r] = zh
        gates(zh, m_ref[pl.ds(r, 1), :], wt_ref, bp_ref, scr_a, scr_b, r)
        return 0
    lax.fori_loop(0, RB, row, 0, unroll=UN)
    ship(step, [(scr_a, st_a, ac_ref, (la, sa, ra), True), (scr_b, st_b, bf_ref, (lb, sb, rb_), False)])

    @pl.when(step < 4)
    def _():
        ao_ref[...] = st_a[lax.rem(step, 2)]
        bo1_ref[...] = st_b[lax.rem(step, 2)]


def post_row(x, zh, lnm_ref, wot_ref, wo_ref, bo_ref, wgt_ref, bg_ref, dz):
    xn, rstd = norm(x)
    xh = (xn * lnm_ref[0] + lnm_ref[1]).astype(BF16)
    u = dot(wot_ref[...], xh) + bo_ref[...]
    g = sig(dot(wgt_ref[...], zh) + bg_ref[...])
    d_pg = dz * u * (g * (1.0 - g))
    d_upd = dz * g
    d_bf = d_upd.astype(BF16)
    d_xh = dot(wo_ref[...], d_bf)
    dx = norm_bwd(d_xh, xn, rstd, lnm_ref[0])
    return xh, xn, u, g, d_pg, d_upd, d_bf, d_xh, dx


def post_grads(parts, dwo_ref, vec_ref):
    xh, xn, d_pg, d_upd, d_bf, d_xh = parts
    dwo_ref[...] += dot_t(xh, d_bf)
    vec_ref[0] += d_upd
    vec_ref[1] += d_xh * xn
    vec_ref[2] += d_xh
    vec_ref[3] += d_pg


def zero(*refs):
    for ref in refs:
        ref[...] = jnp.zeros_like(ref)


def post1_kernel(x_ref, zh_ref, zm_ref, dz_ref, dzo_ref, lnm_ref, wot_ref, wo_ref, bo_ref, wgt_ref, bg_ref,
                 zo_ref, dpg_ref, dzt_ref, dwo_ref, vec_ref, dxf_ref, scr_x, scr_d, st, lsem, ssem, rsem):
    step = pl.program_id(0)

    @pl.when(step == 0)
    def _():
        greet((0,))
        zero(dwo_ref, vec_ref)
    unpack(x_ref, scr_x)

    @pl.when(step >= 4)
    def _():
        def row(r, _):
            dz = load_t(dzo_ref, r)
            res = post_row(get_row(scr_x, r), zh_ref[r], lnm_ref, wot_ref, wo_ref, bo_ref, wgt_ref, bg_ref, dz)
            put_row(scr_d, r, res[-1])
            return 0
        lax.fori_loop(0, RB, row, 0, unroll=UN)

    @pl.when(step < 4)
    def _():
        def row(r, _):
            dz = load_t(dz_ref, r)
            dzt_ref[r] = dz.astype(BF16)
            xh, xn, u, g, d_pg, d_upd, d_bf, d_xh, dx = post_row(get_row(scr_x, r), zh_ref[r], lnm_ref, wot_ref, wo_ref, bo_ref, wgt_ref, bg_ref, dz)
            put_row(scr_d, r, dx)
            dpg_ref[r] = d_pg.astype(BF16)
            store_t(zo_ref, r, zm_ref[r].astype(F32) + g * u)
            post_grads((xh, xn, d_pg, d_upd, d_bf, d_xh), dwo_ref, vec_ref)
            return 0
        lax.fori_loop(0, RB, row, 0, unroll=UN)
    ship(step, [(scr_d, st, dxf_ref, (lsem, ssem, rsem), False)])


def pre_bwd_row(r, z, zh, m, d_pg, scr_a, scr_b, ln_ref, wt_ref, w_ref, bp_ref, dp_ref, dwp_ref, vec_ref, base):
    for q, scr in ((0, scr_a), (1, scr_b)):
        p = dot(wt_ref[q * 256:(q + 1) * 256, :], zh)
        s = sig(p[0:128] + bp_ref[2 * q])
        v = p[128:256] + bp_ref[2 * q + 1]
        d_s = get_row(scr, r) * m
        d_v = d_s * s
        d_g = d_v * v * (1.0 - s)
        dp_ref[q * 256:q * 256 + 128, :] = d_g.astype(BF16)
        dp_ref[q * 256 + 128:q * 256 + 256, :] = d_v.astype(BF16)
        vec_ref[base + 2 * q] += d_g
        vec_ref[base + 2 * q + 1] += d_v
    dp_ref[512:640, :] = d_pg
    dp = dp_ref[...]
    dwp_ref[...] += dot_t(dp, zh)
    d_zh = dot(w_ref[...], dp)
    zn, rstd = norm(z)
    vec_ref[base + 4] += d_zh * zn
    vec_ref[base + 5] += d_zh
    return norm_bwd(d_zh, zn, rstd, ln_ref[0])


def midb_kernel(da_ref, db_ref, zh1_ref, zm_ref, m_ref, dpg1_ref, dzt_ref, x0_ref, zh0_ref,
                ln_ref, wt_ref, w_ref, bp_ref, lnm_ref, wot_ref, wo_ref, bo_ref, wgt_ref, bg_ref,
                dzm_ref, dx_ref, dpg0_ref, dwp_ref, dwo_ref, vec_ref, vec2_ref, scr_a, scr_b, scr_x, scr_d, dp_ref):
    @pl.when(pl.program_id(0) == 0)
    def _():
        zero(dwp_ref, dwo_ref, vec_ref, vec2_ref)
    unpack(da_ref, scr_a)
    unpack(db_ref, scr_b)
    unpack(x0_ref, scr_x)

    def row(r, _):
        dz_norm = pre_bwd_row(r, zm_ref[r].astype(F32), zh1_ref[r], m_ref[pl.ds(r, 1), :], dpg1_ref[r], scr_a, scr_b,
                              ln_ref, wt_ref, w_ref, bp_ref, dp_ref, dwp_ref, vec_ref, 0)
        dzm = (dzt_ref[r].astype(F32) + dz_norm).astype(BF16)
        dzm_ref[r] = dzm
        xh, xn, u, g, d_pg, d_upd, d_bf, d_xh, dx = post_row(get_row(scr_x, r), zh0_ref[r], lnm_ref, wot_ref, wo_ref, bo_ref, wgt_ref, bg_ref, dzm.astype(F32))
        put_row(scr_d, r, dx)
        dpg0_ref[r] = d_pg.astype(BF16)
        post_grads((xh, xn, d_pg, d_upd, d_bf, d_xh), dwo_ref, vec2_ref)
        return 0
    lax.fori_loop(0, RB, row, 0, unroll=UN)
    pack(scr_d, dx_ref)


def last_kernel(da_ref, db_ref, zh_ref, zt_ref, m_ref, dpg_ref, dzm_ref, ln_ref, wt_ref, w_ref, bp_ref,
                dz_ref, dwp_ref, vec_ref, scr_a, scr_b, dp_ref):
    @pl.when(pl.program_id(0) == 0)
    def _():
        zero(dwp_ref, vec_ref)
    unpack(da_ref, scr_a)
    unpack(db_ref, scr_b)

    def row(r, _):
        dz_norm = pre_bwd_row(r, zt_ref[r].astype(F32), zh_ref[r], m_ref[pl.ds(r, 1), :], dpg_ref[r], scr_a, scr_b,
                              ln_ref, wt_ref, w_ref, bp_ref, dp_ref, dwp_ref, vec_ref, 0)
        store_t(dz_ref, r, dzm_ref[r].astype(F32) + dz_norm)
        return 0
    lax.fori_loop(0, RB, row, 0, unroll=UN)


def sds(shape, dtype):
    return jax.ShapeDtypeStruct(shape, dtype)


def full(shape):
    nd = len(shape)
    return pl.BlockSpec(shape, lambda *_: (0,) * nd)


def rows_spec(shape, fn):
    return pl.BlockSpec((RB,) + shape, lambda i: (fn(i),) + (0,) * len(shape))


def cm_spec(fn):
    return pl.BlockSpec((C, RB, N), lambda i: (0, fn(i), 0))


def scr():
    return pltpu.VMEM((2, C * SP, 128), F32)


ANY = pl.BlockSpec(memory_space=pl.ANY)


def call(kernel, grid, in_specs, out_specs, out_shape, scratch, name, cid=None):
    return pl.pallas_call(
        kernel, name=name, out_shape=out_shape, grid=(grid,), in_specs=in_specs, out_specs=out_specs, scratch_shapes=scratch,
        compiler_params=pltpu.CompilerParams(dimension_semantics=("arbitrary",), vmem_limit_bytes=60 << 20, collective_id=cid, has_side_effects=cid is not None))


def reduce_kernel(dwp0_ref, dwo0_ref, pre0_ref, post0_ref, dwp1_ref, dwo1_ref, pre1_ref, post1_ref, out_ref, acc, got0, got1, got2, got3, send, recv):
    greet((0, 1, 2, 3))
    parts = ((dwp0_ref, dwo0_ref, pre0_ref, post0_ref), (dwp1_ref, dwo1_ref, pre1_ref, post1_ref))
    for k, (dwp, dwo, vpre, vpost) in enumerate(parts):
        acc[784 * k:784 * k + 640, :] = dwp[...]
        acc[784 * k + 640:784 * k + 768, :] = dwo[...]
        rows = [jnp.sum(jnp.transpose(v[q]), axis=0, keepdims=True) for v, n in ((vpre, 6), (vpost, 4)) for q in range(n)]
        acc[784 * k + 768:784 * k + 784, :] = jnp.concatenate(rows + [jnp.zeros((6, C), F32)], axis=0)
    acc[1568:GROWS, :] = jnp.zeros((GROWS - 1568, C), F32)
    got = (got0, got1, got2, got3)
    spans = [[r0, n] for r0, n, _ in CHUNKS]
    for st in range(4):
        copies = []
        base = 0
        for ch, (_, _, order) in enumerate(CHUNKS):
            lo, n = spans[ch]
            half = n // 2
            bit = partner(order[st])[0]
            give = pl.multiple_of(lo + (1 - bit) * half, 8)
            keep = pl.multiple_of(lo + bit * half, 8)
            land = got[st].at[pl.ds(base, half), :]
            cp = remote(acc.at[pl.ds(give, half), :], land, send.at[st, ch], recv.at[st, ch], order[st])
            cp.start()
            copies.append((cp, keep, half, base))
            spans[ch] = [keep, half]
            base += half
        for cp, keep, half, base in copies:
            cp.wait()
            acc[pl.ds(keep, half), :] += got[st][base:base + half, :]
    for lo, n in spans:
        out_ref[pl.ds(lo, n), :] = acc[pl.ds(lo, n), :]
    for st in (3, 2, 1, 0):
        copies = []
        for ch, (_, _, order) in enumerate(CHUNKS):
            lo, n = spans[ch]
            bit = partner(order[st])[0]
            seg = out_ref.at[pl.ds(pl.multiple_of(lo, 8), n), :]
            cp = remote(seg, seg, send.at[4 + st, ch], recv.at[4 + st, ch], order[st])
            cp.start()
            copies.append(cp)
            spans[ch] = [lo - bit * n, 2 * n]
        for cp in copies:
            cp.wait()


def reduce_all(*g):
    vm = pl.BlockSpec(memory_space=pltpu.VMEM)
    return pl.pallas_call(
        reduce_kernel, name="reduce", out_shape=sds((GROWS, C), F32), in_specs=[vm] * 8, out_specs=vm,
        scratch_shapes=[pltpu.VMEM((GROWS, C), F32)] + [pltpu.VMEM((GROWS >> (k + 1), C), F32) for k in range(4)]
        + [pltpu.SemaphoreType.DMA((8, 3)), pltpu.SemaphoreType.DMA((8, 3))],
        compiler_params=pltpu.CompilerParams(collective_id=0, has_side_effects=True))(*g)


def solution(mesh):
    def local_step(z_pair, pair_mask, dz_out, ln_in, w_proj, b_proj, ln_mid, w_out, b_out):
        mask = pair_mask[0].reshape(64, 2, 2, 64).transpose(0, 2, 1, 3).reshape(64, N).astype(F32)

        def wide(v):
            return jnp.broadcast_to(v.astype(F32)[..., None], v.shape + (N,))

        lni = wide(ln_in)
        lnm = wide(ln_mid)
        bp = wide(b_proj.reshape(2, 5, C))
        bo = wide(b_out)
        wt = jnp.swapaxes(w_proj, 1, 2)
        wot = jnp.swapaxes(w_out, 1, 2)

        same = lambda i: i
        cm_all = sds((C, 128, N), BF16)
        cm_full = sds((C, N, N), BF16)
        cm_own = sds((C, 64, N), BF16)
        rt_all = sds((128, C, N), BF16)
        rt_own = sds((64, C, N), BF16)
        vm = pl.BlockSpec(memory_space=pltpu.VMEM)

        a0, zh0, zt0, mask_all, a0f, b0f = call(
            pre_kernel, 8, [ANY, vm, full((2, C, N)), full((512, C)), full((5, C, N))],
            [cm_spec(rb), rows_spec((C, N), rb), rows_spec((C, N), rb), vm, ANY, ANY],
            [cm_all, rt_all, rt_all, sds((128, N), F32), cm_full, cm_full],
            [scr(), scr(), pltpu.VMEM((128, N), F32), pltpu.VMEM((128, N, C), BF16)] + [pltpu.SemaphoreType.DMA((4,))] * 3 + [pltpu.SemaphoreType.DMA((3,))] + ship_scratch() * 2,
            "pre", 1)(z_pair[0], mask, lni[0], wt[0, :512], bp[0])
        dz_own, a0 = lax.optimization_barrier((dz_out[0], a0))
        dz_oth = lax.ppermute(dz_own, "dap", SWAP_X)
        x0 = jnp.einsum("cik,cjk->cij", a0, b0f, preferred_element_type=F32)

        sm = [full((2, C, N)), full((C, C)), full((C, N)), full((C, C)), full((C, N))]
        zm, zh1, a1o, b1o, a1c, b1f = call(
            mid_kernel, 8,
            [cm_spec(rb), rows_spec((C, N), rb), rows_spec((C, N), rb), rows_spec((N,), rb)] + sm + [full((2, C, N)), full((512, C)), full((5, C, N))],
            [rows_spec((C, N), rb), rows_spec((C, N), rb), cm_spec(first4), cm_spec(first4), ANY, ANY],
            [rt_all, rt_all, cm_own, cm_own, sds((C, N, 128), BF16), cm_full],
            [scr(), scr(), scr()] + ship_scratch()[:0] + [pltpu.VMEM((2, C, RB, N), BF16)] + ship_scratch()[1:] + ship_scratch(),
            "mid", 2)(x0, zh0, zt0, mask_all, lnm[0], wot[0], bo[0], wt[0, 512:], bp[0, 4], lni[1], wt[1, :512], bp[1])
        x1 = jnp.einsum("cki,ckj->cij", a1c, b1f, preferred_element_type=F32)

        late = lambda i: lax.max(i - 4, 0)
        smb = [full((2, C, N)), full((C, C)), full((C, C)), full((C, N)), full((C, C)), full((C, N))]
        zo, dpg1, dzt, dwo1, vec1, dx1f = call(
            post1_kernel, 8,
            [cm_spec(rb), rows_spec((C, N), rb), rows_spec((C, N), rb), rows_spec((N, C), first4), rows_spec((N, C), late)] + smb,
            [rows_spec((N, C), first4), rows_spec((C, N), first4), rows_spec((C, N), first4), full((C, C)), full((4, C, N)), ANY],
            [sds((64, N, C), BF16), rt_own, rt_own, sds((C, C), F32), sds((4, C, N), F32), cm_full],
            [scr(), scr()] + ship_scratch(), "post1", 3)(
            x1, zh1, zm, dz_own, dz_oth, lnm[1], wot[1], w_out[1], bo[1], wt[1, 512:], bp[1, 4])
        da1 = jnp.einsum("ckj,cij->cki", b1o, dx1f, preferred_element_type=F32).astype(BF16)
        db1 = jnp.einsum("cki,cij->ckj", a1o, dx1f, preferred_element_type=F32).astype(BF16)

        own = lambda i: i + 4 * partner(1)[0]
        wp = [full((2, C, N)), full((640, C)), full((C, 640)), full((5, C, N))]
        dzm, dx0, dpg0, dwp1, dwo0, vec2, vec3 = call(
            midb_kernel, 4,
            [cm_spec(same), cm_spec(same), rows_spec((C, N), own), rows_spec((C, N), own), rows_spec((N,), own),
             rows_spec((C, N), same), rows_spec((C, N), same), cm_spec(own), rows_spec((C, N), own)] + wp + smb,
            [rows_spec((C, N), same), cm_spec(same), rows_spec((C, N), same), full((640, C)), full((C, C)), full((6, C, N)), full((4, C, N))],
            [rt_own, sds((C, 64, N), BF16), rt_own, sds((640, C), F32), sds((C, C), F32), sds((6, C, N), F32), sds((4, C, N), F32)],
            [scr(), scr(), scr(), scr(), pltpu.VMEM((640, N), BF16)], "midb")(
            da1, db1, zh1, zm, mask_all, dpg1, dzt, x0, zh0, lni[1], wt[1], w_proj[1], bp[1],
            lnm[0], wot[0], w_out[0], bo[0], wt[0, 512:], bp[0, 4])
        dx0c = lax.all_to_all(dx0, "dap", 2, 1, axis_index_groups=QUAD, tiled=True)
        da0 = jnp.einsum("cij,cjk->cik", dx0, b0f, preferred_element_type=F32).astype(BF16)
        db0 = jnp.einsum("cij,cik->cjk", dx0c, a0f, preferred_element_type=F32).astype(BF16)

        dzp, dwp0, vec4 = call(
            last_kernel, 4,
            [cm_spec(same), cm_spec(same), rows_spec((C, N), own), rows_spec((C, N), own), rows_spec((N,), own),
             rows_spec((C, N), same), rows_spec((C, N), same)] + wp,
            [rows_spec((N, C), same), full((640, C)), full((6, C, N))],
            [sds((64, N, C), BF16), sds((640, C), F32), sds((6, C, N), F32)],
            [scr(), scr(), pltpu.VMEM((640, N), BF16)], "last")(
            da0, db0, zh0, zt0, mask_all, dpg0, dzm, lni[0], wt[0], w_proj[0], bp[0])

        g = reduce_all(dwp0, dwo0, vec4, vec3, dwp1, dwo1, vec2, vec1)[:1568].reshape(2, 784, C)
        d_b = jnp.concatenate([g[:, 768:772].reshape(2, 512), g[:, 777]], axis=1)
        return (zo[None], dzp[None], g[:, 772:774], jnp.swapaxes(g[:, :640], 1, 2), d_b, g[:, 775:777], g[:, 640:768], g[:, 774])

    row_spec = P("dp", "dap")
    return jax.shard_map(local_step, mesh=mesh, in_specs=(row_spec, row_spec, row_spec, P(), P(), P(), P(), P(), P()), out_specs=(row_spec, row_spec, P(), P(), P(), P(), P(), P()), check_vma=False)
```

time: 1120 us -> 506 us (0.45)
  Pallas kernels: 0 us -> 330 us
  waiting for transfers between devices: 341 us -> 35.8 us
  other arithmetic: 226 us -> 2.82 us
  matrix products: 224 us -> 83.3 us
  local copies, waits for them, and re-layouts: 175 us -> 46 us
  blocking collectives: 126 us -> 0 us
  between operations: 15 us -> 0.8 us
    pallas_call x0 -> x6, Pallas kernels: none -> 330 us  [the longest x1 106 us: local_step(): call(pre_kernel, 8, [ANY, vm, full((2, C, N)), full((512, C)), full((5, C...]
    dot_general x18 -> x6, matrix products: 224 us -> 83.3 us  [the longest x1 17 us: local_step(): jnp.einsum('ckj,cij->cki', b1o, dx1f, preferred_element_type=F32)]
    reduce_sum x17 -> x0, other arithmetic: 132 us -> none  [the longest x10 59.7 us: layer_norm(): return centered * lax.rsqrt(variance + LN_EPS) * ln_gain + ln_bias]
    all_gather x2 -> x0, waiting for transfers between devices: 130 us -> none  [the longest x1 100 us: local_step(): b_full0 = lax.all_gather(b_rows0, 'dap', axis=1, tiled=True)]
    reduce_scatter x2 -> x0, waiting for transfers between devices: 104 us -> none  [the longest x1 59.7 us: local_step(): lax.psum_scatter(d_bpart0, 'dap', scatter_dimension=1, tiled=True)]
    all_to_all x1 -> x0, blocking collectives: 94.1 us -> none  [local_step(): d_arows1 = lax.all_to_all(d_acols1, 'dap', 1, 2, tiled=True)]
    dot_general x5 -> x0, local copies, waits for them, and re-layouts: 69.1 us -> none  [the longest x1 24.3 us: local_step(): jnp.einsum('pkic,pijc->pkjc', a_cols1, d_trib1, preferred_element_type=jn...]
    all_gather x2 -> x0, local copies, waits for them, and re-layouts: 45.9 us -> none  [the longest x1 23.4 us: local_step(): b_full0 = lax.all_gather(b_rows0, 'dap', axis=1, tiled=True)]
  transfers between devices with their start and end apart: 6 -> 2, of which waited for: 6 -> 1; matrix products, arithmetic and copies ran while one was open for 12% -> 10% of each run, Pallas kernels for 0% -> 13%
where the time goes in v1:
time: 506 us; the launch traced here: 505 us
  Pallas kernels  330 us (65%)
  matrix products  83.3 us (16%)
  local copies, waits for them, and re-layouts  46 us (9%)
  waiting for transfers between devices  35.8 us (7%)
  starting transfers between devices  5.99 us (1%)
    pallas_call x1, Pallas kernels, local_step(): call(pre_kernel, 8, [ANY, vm, full((2, C, N)), full((512, C)), full((5, C...  106 us
    pallas_call x1, Pallas kernels, local_step(): call(mid_kernel, 8, [cm_spec(rb), rows_spec((C, N), rb), rows_spec((C, N)...  64.4 us
    pallas_call x1, Pallas kernels, local_step(): call(midb_kernel, 4, [cm_spec(same), cm_spec(same), rows_spec((C, N), own...  55.6 us
    pallas_call x1, Pallas kernels, local_step(): call(post1_kernel, 8, [cm_spec(rb), rows_spec((C, N), rb), rows_spec((C,...  40.9 us
    all_to_all x1, waiting for transfers between devices, local_step(): dx0c = lax.all_to_all(dx0, 'dap', 2, 1, axis_index_groups=QUAD, tiled=True)  35.8 us
    pallas_call x1, Pallas kernels, local_step(): call(last_kernel, 4, [cm_spec(same), cm_spec(same), rows_spec((C, N), own...  35.4 us
    pallas_call x1, Pallas kernels, reduce_all(): pl.pallas_call(reduce_kernel, name='reduce', out_shape=sds((GROWS, C), F3...  27.8 us
    dot_general x1, matrix products, local_step(): jnp.einsum('ckj,cij->cki', b1o, dx1f, preferred_element_type=F32)  17 us
  transfers between devices with their start and end apart: 2, of which 1 were waited for; matrix products, arithmetic and copies ran while one was open for 10% of the time, Pallas kernels for 13%

profile of v1, /device:TPU:0, one launch (start us, length us, event | category | flops | bytes accessed | tf_op | source)
XLA Modules:
  0.0 504.7 jit_solution(13517492591101208568)
XLA Ops:
  0.7 1.2 copy.44
  5.8 1.0 broadcast_in_dim.65.bp_ref
  7.6 106.0 %pre.1 = (bf16[128,128,256]{2,1,0:T(8,128)(2,1)}, bf16[128,128,256]{2,1,0:T(8,128)(2,1)}, bf16[128,128,256]{2,1,0:T(8,128)(2,1)}, f32[128,256]{1,0:T(8,128)}, bf...) custom-call(bf16[64,256,128]{2,1,0:T(8,128)(2,1)} %bitcast.82, f32[64,256]{1,0:T(8,128)} %convert_element_type.50.m_ref, ...), custom_call_target="tpu_custom_call" | custom-call | tf_op jit(solution)/shard_map/pre/pallas_call | solution.py:492
  113.6 1.1 collective-permute-start
  117.1 14.3 %fusion.2.x_ref.x0_ref = f32[128,128,256]{2,1,0:T(8,128)} fusion(bf16[128,128,256]{2,1,0:T(8,128)(2,1)} %get-tuple-element.39, bf16[128,256,256]{2,1,0:T(8,128)(2,1)} %get-tuple-element.40), kind=kOutput, calls=%fused_computation.33 | convolution fusion | flops 2147483648 | bytes 41943040 | tf_op jit(solution)/shard_map/cik,cjk->cij/dot_general | solution.py:500
  131.4 1.1 broadcast_in_dim.75.bp_ref
  135.5 64.4 %mid.1 = (bf16[128,128,256]{2,1,0:T(8,128)(2,1)}, bf16[128,128,256]{2,1,0:T(8,128)(2,1)}, bf16[128,64,256]{2,1,0:T(8,128)(2,1)}, bf16[128,64,256]{2,1,0:T(8,128)...) custom-call(f32[128,128,256]{2,1,0:T(8,128)} %fusion.2.x_ref.x0_ref, ...), custom_call_target="tpu_custom_call" | custom-call | tf_op jit(solution)/shard_map/mid/pallas_call | solution.py:503
  202.0 15.6 %fusion.3.x_ref = f32[128,128,256]{2,1,0:T(8,128)} fusion(bf16[128,256,128]{2,1,0:T(8,128)(2,1)} %get-tuple-element.44, bf16[128,256,256]{2,1,0:T(8,128)(2,1)} %get-tuple-element.45), kind=kOutput, calls=%fused_computation.34 | convolution fusion | flops 2147483648 | bytes 41943040 | tf_op jit(solution)/shard_map/cki,ckj->cij/dot_general | solution.py:510
  219.9 40.9 %post1.1 = (bf16[64,256,128]{2,1,0:T(8,128)(2,1)}, bf16[64,128,256]{2,1,0:T(8,128)(2,1)}, bf16[64,128,256]{2,1,0:T(8,128)(2,1)}, f32[128,128]{1,0:T(8,128)}, f32...) custom-call(f32[128,128,256]{2,1,0:T(8,128)} %fusion.3.x_ref, ...), custom_call_target="tpu_custom_call" | custom-call | tf_op jit(solution)/shard_map/post1/pallas_call | solution.py:514
  260.8 12.2 %convolution_convert_fusion.2.db_ref = bf16[128,64,256]{2,1,0:T(8,128)(2,1)} fusion(bf16[128,64,256]{2,1,0:T(8,128)(2,1)} %get-tuple-element.52, bf16[128,256,256]{2,1,0:T(8,128)(2,1)} %get-tuple-element.51), kind=kOutput, calls=%fused_computation.2 | convolution fusion | flops 1075838976 | bytes 25165824 | tf_op jit(solution)/shard_map/cki,cij->ckj/dot_general | solution.py:522
  273.1 17.0 %convolution_convert_fusion.3.da_ref = bf16[128,64,256]{2,1,0:T(8,128)(2,1)} fusion(bf16[128,64,256]{2,1,0:T(8,128)(2,1)S(1)} %copy-done, bf16[128,256,256]{2,1,0:T(8,128)(2,1)} %get-tuple-element.51), kind=kOutput, calls=%fused_computation.3 | convolution fusion | flops 1075838976 | bytes 25165824 | tf_op jit(solution)/shard_map/ckj,cij->cki/dot_general | solution.py:521
  290.1 55.6 %midb.1 = (bf16[64,128,256]{2,1,0:T(8,128)(2,1)}, bf16[128,64,256]{2,1,0:T(8,128)(2,1)}, bf16[64,128,256]{2,1,0:T(8,128)(2,1)}, f32[640,128]{1,0:T(8,128)}, f32[...) custom-call(bf16[128,64,256]{2,1,0:T(8,128)(2,1)} %convolution_convert_fusion.3.da_ref, ...), custom_call_target="tpu_custom_call" | custom-call | tf_op jit(solution)/shard_map/midb/pallas_call | solution.py:526
  345.7 7.3 %copy.47 = bf16[128,64,256]{0,1,2:T(8,128)(2,1)} copy(bf16[128,64,256]{2,1,0:T(8,128)(2,1)} %get-tuple-element.55) | data formatting | bytes 8388608 | tf_op jit(solution)/shard_map/midb/pallas_call | solution.py:526
  353.0 4.9 all-to-all-start
  357.9 12.1 %convolution_convert_fusion.1.da_ref = bf16[128,64,256]{2,1,0:T(8,128)(2,1)} fusion(bf16[128,64,256]{2,1,0:T(8,128)(2,1)} %get-tuple-element.55, bf16[128,256,256]{2,1,0:T(8,128)(2,1)} %get-tuple-element.40), kind=kOutput, calls=%fused_computation.1 | convolution fusion | flops 1075838976 | bytes 25165824 | tf_op jit(solution)/shard_map/cij,cjk->cik/dot_general | solution.py:536
  370.0 35.8 %all-to-all-done = bf16[128,64,256]{0,1,2:T(8,128)(2,1)} async-done(((bf16[128,64,256]{0,1,2:T(8,128)(2,1)}), bf16[128,64,256]{0,1,2:T(8,128)(2,1)}, u32[]{:S(2)}, u32[]{:S(2)}) %all-to-all-start) | async-done | bytes 4194336 | tf_op jit(solution)/shard_map/all_to_all | solution.py:535
  405.8 6.9 %copy.49 = bf16[128,4,64,64]{0,3,2,1:T(8,128)(2,1)} copy(bf16[128,4,64,64]{0,2,3,1:T(8,128)(2,1)} %bitcast.26) | data formatting | bytes 8388608 | tf_op jit(solution)/shard_map/all_to_all | solution.py:535
  412.7 7.3 %copy.50 = bf16[128,256,64]{1,2,0:T(8,128)(2,1)} copy(bf16[128,256,64]{0,2,1:T(8,128)(2,1)} %bitcast.79) | data formatting | bytes 8388608 | tf_op jit(solution)/shard_map/all_to_all | solution.py:535
  420.0 12.0 %convolution_convert_fusion.db_ref = bf16[128,64,256]{2,1,0:T(8,128)(2,1)} fusion(bf16[128,256,64]{1,2,0:T(8,128)(2,1)} %copy.50, bf16[128,256,256]{2,1,0:T(8,128)(2,1)} %get-tuple-element.56), kind=kOutput, calls=%fused_computation | convolution fusion | flops 1075838976 | bytes 25165824 | tf_op jit(solution)/shard_map/cij,cik->cjk/dot_general | solution.py:537
  432.0 35.4 %last.1 = (bf16[64,256,128]{2,1,0:T(8,128)(2,1)}, f32[640,128]{1,0:T(8,128)}, f32[6,128,256]{2,1,0:T(8,128)}) custom-call(bf16[128,64,256]{2,1,0:T(8,128)(2,1)} %convolution_convert_fusion.1.da_ref, bf16[128,64,256]{2,1,0:T(8,128)(2,1)} %convolution_convert_fusion.db_ref, bf16[128,128,256]{2,1,0:T(8,128)(2,1)} %get-tuple-element.41.zh_ref.zh0_ref, ...), custom_call_target="tpu_custom_call" | custom-call | tf_op jit(solution)/shard_map/last/pallas_call | solution.py:539
  467.5 27.8 %reduce.5 = f32[1664,128]{1,0:T(8,128)} custom-call(f32[640,128]{1,0:T(8,128)} %get-tuple-element.60.dwp0_ref, f32[128,128]{1,0:T(8,128)} %get-tuple-element.61.dwo0_ref, f32[6,128,256]{2,1,0:T(8,128)} %get-tuple-element.62.pre0_ref, f32[4,128,256]{2,1,0:T(8,128)} %get-tuple-element.63.post0_ref, f32[640,128]{1,0:T(8,128)} %get-tuple-element.64.dwp1_ref, ...), custom_call_target="tpu_custom_call" | custom-call | tf_op jit(solution)/shard_map/reduce/pallas_call | solution.py:463
  495.3 1.2 slice.138
  498.3 1.1 copy.52
  500.0 4.7 copy.62
  (46 shorter events, 17.1 us)
Async XLA Ops:
  0.6 116.4 %copy-start.3 = (bf16[2,2,128]{2,1,0:T(2,128)(2,1)S(1)}, bf16[2,2,128]{2,1,0:T(2,128)(2,1)}, u32[]{:S(2)}) copy-start(bf16[2,2,128]{2,1,0:T(2,128)(2,1)} %param.15) | copy-start | bytes 3076
  0.6 116.4 %copy-start.4 = (bf16[2,128]{1,0:T(2,128)(2,1)S(1)}, bf16[2,128]{1,0:T(2,128)(2,1)}, u32[]{:S(2)}) copy-start(bf16[2,128]{1,0:T(2,128)(2,1)} %param.17) | copy-start | bytes 1540
  113.6 104.1 %collective-permute-start = (bf16[64,256,128]{2,1,0:T(8,128)(2,1)}, bf16[64,256,128]{2,1,0:T(8,128)(2,1)}, u32[]{:S(2)}, u32[]{:S(2)}) collective-permute-start(bf16[64,256,128]{2,1,0:T(8,128)(2,1)} %bitcast.80), channel_id=1, source_target_pairs={{0,2},{2,0},{1,3},{3,1},{4,6},{6,4},{5,7},{7,5},{8,10},{10,8},{9,1... | collective-permute-start | bytes 12582920 | tf_op jit(solution)/shard_map/ppermute | solution.py:499
  135.5 64.4 %copy-start.2 = (bf16[2,128,128]{2,1,0:T(8,128)(2,1)S(1)}, bf16[2,128,128]{2,1,0:T(8,128)(2,1)}, u32[]{:S(2)}) copy-start(bf16[2,128,128]{2,1,0:T(8,128)(2,1)} %param.16) | copy-start | bytes 196612
  135.5 65.8 %copy-start.1 = (bf16[2,128,640]{2,1,0:T(8,128)(2,1)S(1)}, bf16[2,128,640]{2,1,0:T(8,128)(2,1)}, u32[]{:S(2)}) copy-start(bf16[2,128,640]{2,1,0:T(8,128)(2,1)} %param.13) | copy-start | bytes 983044
  260.8 12.2 %copy-start = (bf16[128,64,256]{2,1,0:T(8,128)(2,1)S(1)}, bf16[128,64,256]{2,1,0:T(8,128)(2,1)}, u32[]{:S(2)}) copy-start(bf16[128,64,256]{2,1,0:T(8,128)(2,1)} %get-tuple-element.50) | copy-start | bytes 12582916
  353.0 52.7 %all-to-all-start = ((bf16[128,64,256]{0,1,2:T(8,128)(2,1)}), bf16[128,64,256]{0,1,2:T(8,128)(2,1)}, u32[]{:S(2)}, u32[]{:S(2)}) async-start(bf16[128,64,256]{0,1,2:T(8,128)(2,1)} %copy.47), calls=%async_computation | async-start | bytes 8388608 | tf_op jit(solution)/shard_map/all_to_all | solution.py:535

commit v2 on v1

--- a/solution.py
+++ b/solution.py
@@ -9,12 +9,12 @@
 LN_EPS = 1e-5
 RB = 16
 SP = 17
-UN = 4
+UN = 8
+GR = 4
 F32 = jnp.float32
 BF16 = jnp.bfloat16
 C = 128
 N = 256
-QUAD = [[0, 2, 1, 3]]
 SWAP_X = [(0, 2), (2, 0), (1, 3), (3, 1)]
 
 
@@ -53,8 +53,13 @@
 
 
 def store_t(ref, r, val):
-    t = perm_cols(jnp.transpose(val)).astype(BF16)
-    ref[r] = t
+    ref[r] = perm_cols(jnp.transpose(val))
+
+
+def by_chip(v):
+    v0, v1 = v[:, :128], v[:, 128:]
+    low = lax.broadcasted_iota(jnp.int32, (C, 128), 1) < 64
+    return jnp.concatenate([jnp.where(low, v0, pltpu.roll(v1, 64, 1)), jnp.where(low, pltpu.roll(v0, 64, 1), v1)], axis=1)
 
 
 def put_row(scr, r, val):
@@ -86,11 +91,19 @@
     lax.fori_loop(0, C // 8, body, 0)
 
 
-def gates(zh, m, wt, bp, scr_a, scr_b, r):
-    pa = dot(wt[0:256, :], zh)
-    put_row(scr_a, r, sig(pa[0:128] + bp[0]) * (pa[128:256] + bp[1]) * m)
-    pb = dot(wt[256:512, :], zh)
-    put_row(scr_b, r, sig(pb[0:128] + bp[2]) * (pb[128:256] + bp[3]) * m)
+def gates(zh, m, wt, bp, scr_a, scr_b, g_ref, r):
+    p = dot(wt[...], zh)
+    put_row(scr_a, r, sig(p[0:128] + bp[0]) * (p[128:256] + bp[1]) * m)
+    put_row(scr_b, r, sig(p[256:384] + bp[2]) * (p[384:512] + bp[3]) * m)
+    g_ref[r] = sig(p[512:640] + bp[4])
+
+
+def groups(body):
+    lax.fori_loop(0, RB // GR, body, 0)
+
+
+def halves(v):
+    return v[:, :128] + v[:, 128:]
 
 
 CHUNKS = ((0, 640, (0, 1, 2, 3)), (640, 512, (0, 2, 3, 1)), (1152, 512, (0, 3, 1, 2)))
@@ -175,7 +188,7 @@
     return [pltpu.VMEM((2, C, RB, N), BF16), pltpu.SemaphoreType.DMA((2,)), pltpu.SemaphoreType.DMA((2,)), pltpu.SemaphoreType.DMA((8,))]
 
 
-def pre_kernel(z_ref, m_ref, ln_ref, wt_ref, bp_ref, a_ref, zh_ref, zt_ref, mall_ref, af_ref, bf_ref,
+def pre_kernel(z_ref, m_ref, ln_ref, wt_ref, bp_ref, a_ref, zh_ref, zt_ref, g_ref, mall_ref, af_ref, bf_ref,
                scr_a, scr_b, mbuf, zbuf, zloc, zsend, zrecv, msem, st_a, la, sa, ra, st_b, lb, sb, rb_):
     step = pl.program_id(0)
     xb = partner(1)[0]
@@ -219,7 +232,7 @@
         zn, _ = norm(zt)
         zh = (zn * ln_ref[0] + ln_ref[1]).astype(BF16)
         zh_ref[r] = zh
-        gates(zh, mbuf[pl.ds(rb(step) * RB + r, 1), :], wt_ref, bp_ref, scr_a, scr_b, r)
+        gates(zh, mbuf[pl.ds(rb(step) * RB + r, 1), :], wt_ref, bp_ref, scr_a, scr_b, g_ref, r)
         return 0
     lax.fori_loop(0, RB, row, 0, unroll=UN)
     ship(step, [(scr_a, st_a, af_ref, (la, sa, ra), False), (scr_b, st_b, bf_ref, (lb, sb, rb_), False)])
@@ -230,8 +243,8 @@
         mall_ref[...] = mbuf[...]
 
 
-def mid_kernel(x_ref, zh_ref, zt_ref, m_ref, lnm_ref, wot_ref, bo_ref, wgt_ref, bg_ref, ln_ref, wt_ref, bp_ref,
-               zm_ref, zh1_ref, ao_ref, bo1_ref, ac_ref, bf_ref, scr_x, scr_a, scr_b, st_a, la, sa, ra, st_b, lb, sb, rb_):
+def mid_kernel(x_ref, g_ref, zt_ref, m_ref, lnm_ref, wot_ref, bo_ref, ln_ref, wt_ref, bp_ref,
+               zm_ref, zh1_ref, g1_ref, ao_ref, bo1_ref, ac_ref, bf_ref, scr_x, scr_a, scr_b, st_a, la, sa, ra, st_b, lb, sb, rb_):
     step = pl.program_id(0)
 
     @pl.when(step == 0)
@@ -243,13 +256,12 @@
         xn, _ = norm(get_row(scr_x, r))
         xh = (xn * lnm_ref[0] + lnm_ref[1]).astype(BF16)
         u = dot(wot_ref[...], xh) + bo_ref[...]
-        g = sig(dot(wgt_ref[...], zh_ref[r]) + bg_ref[...])
-        zm = (zt_ref[r].astype(F32) + g * u).astype(BF16)
+        zm = (zt_ref[r].astype(F32) + g_ref[r] * u).astype(BF16)
         zm_ref[r] = zm
         zn, _ = norm(zm.astype(F32))
         zh = (zn * ln_ref[0] + ln_ref[1]).astype(BF16)
         zh1_ref[r] = zh
-        gates(zh, m_ref[pl.ds(r, 1), :], wt_ref, bp_ref, scr_a, scr_b, r)
+        gates(zh, m_ref[pl.ds(r, 1), :], wt_ref, bp_ref, scr_a, scr_b, g1_ref, r)
         return 0
     lax.fori_loop(0, RB, row, 0, unroll=UN)
     ship(step, [(scr_a, st_a, ac_ref, (la, sa, ra), True), (scr_b, st_b, bf_ref, (lb, sb, rb_), False)])
@@ -260,26 +272,25 @@
         bo1_ref[...] = st_b[lax.rem(step, 2)]
 
 
-def post_row(x, zh, lnm_ref, wot_ref, wo_ref, bo_ref, wgt_ref, bg_ref, dz):
+def post_row(x, g, lnm_ref, wot_ref, wo_ref, bo_ref, dz):
     xn, rstd = norm(x)
     xh = (xn * lnm_ref[0] + lnm_ref[1]).astype(BF16)
     u = dot(wot_ref[...], xh) + bo_ref[...]
-    g = sig(dot(wgt_ref[...], zh) + bg_ref[...])
     d_pg = dz * u * (g * (1.0 - g))
     d_upd = dz * g
     d_bf = d_upd.astype(BF16)
     d_xh = dot(wo_ref[...], d_bf)
     dx = norm_bwd(d_xh, xn, rstd, lnm_ref[0])
-    return xh, xn, u, g, d_pg, d_upd, d_bf, d_xh, dx
-
-
-def post_grads(parts, dwo_ref, vec_ref):
-    xh, xn, d_pg, d_upd, d_bf, d_xh = parts
-    dwo_ref[...] += dot_t(xh, d_bf)
-    vec_ref[0] += d_upd
-    vec_ref[1] += d_xh * xn
-    vec_ref[2] += d_xh
-    vec_ref[3] += d_pg
+    return xh, xn, u, d_pg, d_upd, d_bf, d_xh, dx
+
+
+def post_vecs(vec_ref, d_upd, d_xh, xn, d_pg):
+    for q, v in enumerate((d_upd, d_xh * xn, d_xh, d_pg)):
+        vec_ref[q] += halves(v)
+
+
+def add_outer(acc_ref, left, right):
+    acc_ref[...] += dot(jnp.concatenate(left, axis=1), jnp.transpose(jnp.concatenate(right, axis=1)))
 
 
 def zero(*refs):
@@ -287,7 +298,7 @@
         ref[...] = jnp.zeros_like(ref)
 
 
-def post1_kernel(x_ref, zh_ref, zm_ref, dz_ref, dzo_ref, lnm_ref, wot_ref, wo_ref, bo_ref, wgt_ref, bg_ref,
+def post1_kernel(x_ref, g_ref, zm_ref, dz_ref, dzo_ref, lnm_ref, wot_ref, wo_ref, bo_ref,
                  zo_ref, dpg_ref, dzt_ref, dwo_ref, vec_ref, dxf_ref, scr_x, scr_d, st, lsem, ssem, rsem):
     step = pl.program_id(0)
 
@@ -301,86 +312,162 @@
     def _():
         def row(r, _):
             dz = load_t(dzo_ref, r)
-            res = post_row(get_row(scr_x, r), zh_ref[r], lnm_ref, wot_ref, wo_ref, bo_ref, wgt_ref, bg_ref, dz)
+            res = post_row(get_row(scr_x, r), g_ref[r], lnm_ref, wot_ref, wo_ref, bo_ref, dz)
             put_row(scr_d, r, res[-1])
             return 0
-        lax.fori_loop(0, RB, row, 0, unroll=UN)
+        lax.fori_loop(0, RB, row, 0, unroll=GR)
 
     @pl.when(step < 4)
     def _():
-        def row(r, _):
-            dz = load_t(dz_ref, r)
-            dzt_ref[r] = dz.astype(BF16)
-            xh, xn, u, g, d_pg, d_upd, d_bf, d_xh, dx = post_row(get_row(scr_x, r), zh_ref[r], lnm_ref, wot_ref, wo_ref, bo_ref, wgt_ref, bg_ref, dz)
-            put_row(scr_d, r, dx)
-            dpg_ref[r] = d_pg.astype(BF16)
-            store_t(zo_ref, r, zm_ref[r].astype(F32) + g * u)
-            post_grads((xh, xn, d_pg, d_upd, d_bf, d_xh), dwo_ref, vec_ref)
+        def group(i, _):
+            left, right = [], []
+            for k in range(GR):
+                r = i * GR + k
+                dz = load_t(dz_ref, r)
+                dzt_ref[r] = dz.astype(BF16)
+                g = g_ref[r]
+                xh, xn, u, d_pg, d_upd, d_bf, d_xh, dx = post_row(get_row(scr_x, r), g, lnm_ref, wot_ref, wo_ref, bo_ref, dz)
+                put_row(scr_d, r, dx)
+                dpg_ref[r] = d_pg.astype(BF16)
+                zo_ref[r] = (zm_ref[r].astype(F32) + g * u).astype(BF16)
+                post_vecs(vec_ref, d_upd, d_xh, xn, d_pg)
+                left.append(xh)
+                right.append(d_bf)
+            add_outer(dwo_ref, left, right)
             return 0
-        lax.fori_loop(0, RB, row, 0, unroll=UN)
+        groups(group)
     ship(step, [(scr_d, st, dxf_ref, (lsem, ssem, rsem), False)])
 
 
-def pre_bwd_row(r, z, zh, m, d_pg, scr_a, scr_b, ln_ref, wt_ref, w_ref, bp_ref, dp_ref, dwp_ref, vec_ref, base):
+def pre_bwd_row(r, k, z, zh, m, d_pg, scr_a, scr_b, ln_ref, wt_ref, w_ref, bp_ref, dp_ref, vec_ref):
+    p = dot(wt_ref[0:512, :], zh)
+    cols = slice(k * N, k * N + N)
     for q, scr in ((0, scr_a), (1, scr_b)):
-        p = dot(wt_ref[q * 256:(q + 1) * 256, :], zh)
-        s = sig(p[0:128] + bp_ref[2 * q])
-        v = p[128:256] + bp_ref[2 * q + 1]
+        s = sig(p[q * 256:q * 256 + 128] + bp_ref[2 * q])
+        v = p[q * 256 + 128:q * 256 + 256] + bp_ref[2 * q + 1]
         d_s = get_row(scr, r) * m
         d_v = d_s * s
         d_g = d_v * v * (1.0 - s)
-        dp_ref[q * 256:q * 256 + 128, :] = d_g.astype(BF16)
-        dp_ref[q * 256 + 128:q * 256 + 256, :] = d_v.astype(BF16)
-        vec_ref[base + 2 * q] += d_g
-        vec_ref[base + 2 * q + 1] += d_v
-    dp_ref[512:640, :] = d_pg
-    dp = dp_ref[...]
-    dwp_ref[...] += dot_t(dp, zh)
-    d_zh = dot(w_ref[...], dp)
+        dp_ref[q * 256:q * 256 + 128, cols] = d_g.astype(BF16)
+        dp_ref[q * 256 + 128:q * 256 + 256, cols] = d_v.astype(BF16)
+        vec_ref[2 * q] += halves(d_g)
+        vec_ref[2 * q + 1] += halves(d_v)
+    dp_ref[512:640, cols] = d_pg
+    d_zh = dot(w_ref[...], dp_ref[:, cols])
     zn, rstd = norm(z)
-    vec_ref[base + 4] += d_zh * zn
-    vec_ref[base + 5] += d_zh
+    vec_ref[4] += halves(d_zh * zn)
+    vec_ref[5] += halves(d_zh)
     return norm_bwd(d_zh, zn, rstd, ln_ref[0])
 
 
-def midb_kernel(da_ref, db_ref, zh1_ref, zm_ref, m_ref, dpg1_ref, dzt_ref, x0_ref, zh0_ref,
-                ln_ref, wt_ref, w_ref, bp_ref, lnm_ref, wot_ref, wo_ref, bo_ref, wgt_ref, bg_ref,
-                dzm_ref, dx_ref, dpg0_ref, dwp_ref, dwo_ref, vec_ref, vec2_ref, scr_a, scr_b, scr_x, scr_d, dp_ref):
-    @pl.when(pl.program_id(0) == 0)
-    def _():
+def midb_kernel(da_ref, db_ref, zh1_ref, zm_ref, m_ref, dpg1_ref, dzt_ref, x0_ref, g0_ref,
+                ln_ref, wt_ref, w_ref, bp_ref, lnm_ref, wot_ref, wo_ref, bo_ref,
+                dzm_ref, dx_ref, dpg0_ref, dwp_ref, dwo_ref, vec_ref, vec2_ref, dxk_ref, scr_a, scr_b, scr_x, scr_d, dp_ref,
+                scr_e, st, lsem, csend, crecv, xsend, xrecv, rsend, rrecv):
+    step = pl.program_id(0)
+    cbit = partner(0)[0]
+    xbit = partner(1)[0]
+
+    def block(core, chip, k):
+        return dxk_ref.at[:, pl.ds(pl.multiple_of(core * 128 + chip * 64 + k * RB, RB), RB), :]
+
+    def part(k, chip):
+        return st.at[lax.rem(k, 2), :, :, pl.ds(pl.multiple_of(chip * 128, 128), 128)]
+
+    def here(k):
+        return pltpu.make_async_copy(part(k, xbit), block(cbit, xbit, k), lsem.at[lax.rem(k, 2)])
+
+    def to_core(k):
+        return remote(part(k, xbit), block(cbit, xbit, k), csend.at[lax.rem(k, 2)], crecv.at[k], 0)
+
+    def to_chip(k):
+        return remote(part(k, 1 - xbit), block(cbit, xbit, k), xsend.at[lax.rem(k, 2)], xrecv.at[k], 1)
+
+    def relay(k):
+        blk = block(cbit, 1 - xbit, k)
+        return remote(blk, blk, rsend.at[k], rrecv.at[k], 0)
+
+    def settle(k):
+        here(k).wait()
+        to_core(k).wait_send()
+        to_chip(k).wait_send()
+
+    @pl.when(step == 0)
+    def _():
+        greet((0, 1))
         zero(dwp_ref, dwo_ref, vec_ref, vec2_ref)
     unpack(da_ref, scr_a)
     unpack(db_ref, scr_b)
     unpack(x0_ref, scr_x)
 
-    def row(r, _):
-        dz_norm = pre_bwd_row(r, zm_ref[r].astype(F32), zh1_ref[r], m_ref[pl.ds(r, 1), :], dpg1_ref[r], scr_a, scr_b,
-                              ln_ref, wt_ref, w_ref, bp_ref, dp_ref, dwp_ref, vec_ref, 0)
-        dzm = (dzt_ref[r].astype(F32) + dz_norm).astype(BF16)
-        dzm_ref[r] = dzm
-        xh, xn, u, g, d_pg, d_upd, d_bf, d_xh, dx = post_row(get_row(scr_x, r), zh0_ref[r], lnm_ref, wot_ref, wo_ref, bo_ref, wgt_ref, bg_ref, dzm.astype(F32))
-        put_row(scr_d, r, dx)
-        dpg0_ref[r] = d_pg.astype(BF16)
-        post_grads((xh, xn, d_pg, d_upd, d_bf, d_xh), dwo_ref, vec2_ref)
+    def group(i, _):
+        left, right, zhs = [], [], []
+        for k in range(GR):
+            r = i * GR + k
+            zh = zh1_ref[r]
+            zhs.append(zh)
+            dz_norm = pre_bwd_row(r, k, zm_ref[r].astype(F32), zh, m_ref[pl.ds(r, 1), :], dpg1_ref[r], scr_a, scr_b,
+                                  ln_ref, wt_ref, w_ref, bp_ref, dp_ref, vec_ref)
+            dzm = (dzt_ref[r].astype(F32) + dz_norm).astype(BF16)
+            dzm_ref[r] = dzm
+            xh, xn, u, d_pg, d_upd, d_bf, d_xh, dx = post_row(get_row(scr_x, r), g0_ref[r], lnm_ref, wot_ref, wo_ref, bo_ref, dzm.astype(F32))
+            put_row(scr_d, r, dx)
+            put_row(scr_e, r, by_chip(dx))
+            dpg0_ref[r] = d_pg.astype(BF16)
+            post_vecs(vec2_ref, d_upd, d_xh, xn, d_pg)
+            left.append(xh)
+            right.append(d_bf)
+        add_outer(dwo_ref, left, right)
+        add_outer(dwp_ref, [dp_ref[...]], zhs)
         return 0
-    lax.fori_loop(0, RB, row, 0, unroll=UN)
+    groups(group)
+
+    @pl.when(step >= 2)
+    def _():
+        settle(step - 2)
+    pack(scr_e, st.at[lax.rem(step, 2)])
+    to_chip(step).start()
+    to_core(step).start()
+    here(step).start()
     pack(scr_d, dx_ref)
 
-
-def last_kernel(da_ref, db_ref, zh_ref, zt_ref, m_ref, dpg_ref, dzm_ref, ln_ref, wt_ref, w_ref, bp_ref,
-                dz_ref, dwp_ref, vec_ref, scr_a, scr_b, dp_ref):
+    @pl.when(step >= 2)
+    def _():
+        to_chip(step - 2).wait_recv()
+        relay(step - 2).start()
+
+    @pl.when(step == 3)
+    def _():
+        for k in (2, 3):
+            to_chip(k).wait_recv()
+            relay(k).start()
+            settle(k)
+        for k in range(4):
+            to_core(k).wait_recv()
+            relay(k).wait()
+
+
+def last_kernel(da_ref, db_ref, zh_ref, zt_ref, m_ref, dpg_ref, dzm_ref, zo_ref, ln_ref, wt_ref, w_ref, bp_ref,
+                dz_ref, zout_ref, dwp_ref, vec_ref, scr_a, scr_b, dp_ref):
     @pl.when(pl.program_id(0) == 0)
     def _():
         zero(dwp_ref, vec_ref)
     unpack(da_ref, scr_a)
     unpack(db_ref, scr_b)
 
-    def row(r, _):
-        dz_norm = pre_bwd_row(r, zt_ref[r].astype(F32), zh_ref[r], m_ref[pl.ds(r, 1), :], dpg_ref[r], scr_a, scr_b,
-                              ln_ref, wt_ref, w_ref, bp_ref, dp_ref, dwp_ref, vec_ref, 0)
-        store_t(dz_ref, r, dzm_ref[r].astype(F32) + dz_norm)
+    def group(i, _):
+        zhs = []
+        for k in range(GR):
+            r = i * GR + k
+            zh = zh_ref[r]
+            zhs.append(zh)
+            dz_norm = pre_bwd_row(r, k, zt_ref[r].astype(F32), zh, m_ref[pl.ds(r, 1), :], dpg_ref[r], scr_a, scr_b,
+                                  ln_ref, wt_ref, w_ref, bp_ref, dp_ref, vec_ref)
+            store_t(dz_ref, r, (dzm_ref[r].astype(F32) + dz_norm).astype(BF16))
+            store_t(zout_ref, r, zo_ref[r])
+        add_outer(dwp_ref, [dp_ref[...]], zhs)
         return 0
-    lax.fori_loop(0, RB, row, 0, unroll=UN)
+    groups(group)
 
 
 def sds(shape, dtype):
@@ -471,79 +558,95 @@
     def local_step(z_pair, pair_mask, dz_out, ln_in, w_proj, b_proj, ln_mid, w_out, b_out):
         mask = pair_mask[0].reshape(64, 2, 2, 64).transpose(0, 2, 1, 3).reshape(64, N).astype(F32)
 
-        def wide(v):
-            return jnp.broadcast_to(v.astype(F32)[..., None], v.shape + (N,))
-
-        lni = wide(ln_in)
-        lnm = wide(ln_mid)
-        bp = wide(b_proj.reshape(2, 5, C))
-        bo = wide(b_out)
+        prm = jnp.concatenate([ln_in, ln_mid, b_out[:, None], b_proj.reshape(2, 5, C)], axis=1).astype(F32)
+        prm = jnp.broadcast_to(prm[..., None], (2, 10, C, N))
         wt = jnp.swapaxes(w_proj, 1, 2)
         wot = jnp.swapaxes(w_out, 1, 2)
+
+        def pick(k, *shape):
+            return pl.BlockSpec((None,) + shape, lambda i: (k,) + (0,) * len(shape))
+
+        def vecs(k, n, at):
+            return pl.BlockSpec((None, n, C, N), lambda i: (k, at, 0, 0))
+
+        def ln_s(k):
+            return [vecs(k, 2, 0)]
+
+        def mid_s(k):
+            return [vecs(k, 2, 1)]
+
+        def bias_s(k):
+            return [pl.BlockSpec((None, None, C, N), lambda i: (k, 4, 0, 0))]
+
+        def proj_s(k):
+            return [pick(k, 640, C)]
+
+        def bp_s(k):
+            return [vecs(k, 5, 1)]
 
         same = lambda i: i
         cm_all = sds((C, 128, N), BF16)
         cm_full = sds((C, N, N), BF16)
         cm_own = sds((C, 64, N), BF16)
         rt_all = sds((128, C, N), BF16)
+        rt_f32 = sds((128, C, N), F32)
         rt_own = sds((64, C, N), BF16)
         vm = pl.BlockSpec(memory_space=pltpu.VMEM)
 
-        a0, zh0, zt0, mask_all, a0f, b0f = call(
-            pre_kernel, 8, [ANY, vm, full((2, C, N)), full((512, C)), full((5, C, N))],
-            [cm_spec(rb), rows_spec((C, N), rb), rows_spec((C, N), rb), vm, ANY, ANY],
-            [cm_all, rt_all, rt_all, sds((128, N), F32), cm_full, cm_full],
+        a0, zh0, zt0, g0, mask_all, a0f, b0f = call(
+            pre_kernel, 8, [ANY, vm] + ln_s(0) + proj_s(0) + bp_s(0),
+            [cm_spec(rb), rows_spec((C, N), rb), rows_spec((C, N), rb), rows_spec((C, N), rb), vm, ANY, ANY],
+            [cm_all, rt_all, rt_all, rt_f32, sds((128, N), F32), cm_full, cm_full],
             [scr(), scr(), pltpu.VMEM((128, N), F32), pltpu.VMEM((128, N, C), BF16)] + [pltpu.SemaphoreType.DMA((4,))] * 3 + [pltpu.SemaphoreType.DMA((3,))] + ship_scratch() * 2,
-            "pre", 1)(z_pair[0], mask, lni[0], wt[0, :512], bp[0])
+            "pre", 1)(z_pair[0], mask, prm, wt, prm)
         dz_own, a0 = lax.optimization_barrier((dz_out[0], a0))
         dz_oth = lax.ppermute(dz_own, "dap", SWAP_X)
         x0 = jnp.einsum("cik,cjk->cij", a0, b0f, preferred_element_type=F32)
 
-        sm = [full((2, C, N)), full((C, C)), full((C, N)), full((C, C)), full((C, N))]
-        zm, zh1, a1o, b1o, a1c, b1f = call(
+        zm, zh1, g1, a1o, b1o, a1c, b1f = call(
             mid_kernel, 8,
-            [cm_spec(rb), rows_spec((C, N), rb), rows_spec((C, N), rb), rows_spec((N,), rb)] + sm + [full((2, C, N)), full((512, C)), full((5, C, N))],
-            [rows_spec((C, N), rb), rows_spec((C, N), rb), cm_spec(first4), cm_spec(first4), ANY, ANY],
-            [rt_all, rt_all, cm_own, cm_own, sds((C, N, 128), BF16), cm_full],
-            [scr(), scr(), scr()] + ship_scratch()[:0] + [pltpu.VMEM((2, C, RB, N), BF16)] + ship_scratch()[1:] + ship_scratch(),
-            "mid", 2)(x0, zh0, zt0, mask_all, lnm[0], wot[0], bo[0], wt[0, 512:], bp[0, 4], lni[1], wt[1, :512], bp[1])
+            [cm_spec(rb), rows_spec((C, N), rb), rows_spec((C, N), rb), rows_spec((N,), rb)] + mid_s(0) + [pick(0, C, C)] + bias_s(0) + ln_s(1) + proj_s(1) + bp_s(1),
+            [rows_spec((C, N), rb), rows_spec((C, N), rb), rows_spec((C, N), rb), cm_spec(first4), cm_spec(first4), ANY, ANY],
+            [rt_all, rt_all, rt_f32, cm_own, cm_own, sds((C, N, 128), BF16), cm_full],
+            [scr(), scr(), scr()] + ship_scratch() * 2,
+            "mid", 2)(x0, g0, zt0, mask_all, prm, wot, prm, prm, wt, prm)
         x1 = jnp.einsum("cki,ckj->cij", a1c, b1f, preferred_element_type=F32)
 
         late = lambda i: lax.max(i - 4, 0)
-        smb = [full((2, C, N)), full((C, C)), full((C, C)), full((C, N)), full((C, C)), full((C, N))]
+        smb = lambda k: mid_s(k) + [pick(k, C, C), pick(k, C, C)] + bias_s(k)
         zo, dpg1, dzt, dwo1, vec1, dx1f = call(
             post1_kernel, 8,
-            [cm_spec(rb), rows_spec((C, N), rb), rows_spec((C, N), rb), rows_spec((N, C), first4), rows_spec((N, C), late)] + smb,
-            [rows_spec((N, C), first4), rows_spec((C, N), first4), rows_spec((C, N), first4), full((C, C)), full((4, C, N)), ANY],
-            [sds((64, N, C), BF16), rt_own, rt_own, sds((C, C), F32), sds((4, C, N), F32), cm_full],
+            [cm_spec(rb), rows_spec((C, N), rb), rows_spec((C, N), rb), rows_spec((N, C), first4), rows_spec((N, C), late)] + smb(1),
+            [rows_spec((C, N), first4), rows_spec((C, N), first4), rows_spec((C, N), first4), full((C, C)), full((4, C, C)), ANY],
+            [rt_own, rt_own, rt_own, sds((C, C), F32), sds((4, C, C), F32), cm_full],
             [scr(), scr()] + ship_scratch(), "post1", 3)(
-            x1, zh1, zm, dz_own, dz_oth, lnm[1], wot[1], w_out[1], bo[1], wt[1, 512:], bp[1, 4])
+            x1, g1, zm, dz_own, dz_oth, prm, wot, w_out, prm)
         da1 = jnp.einsum("ckj,cij->cki", b1o, dx1f, preferred_element_type=F32).astype(BF16)
         db1 = jnp.einsum("cki,cij->ckj", a1o, dx1f, preferred_element_type=F32).astype(BF16)
 
         own = lambda i: i + 4 * partner(1)[0]
-        wp = [full((2, C, N)), full((640, C)), full((C, 640)), full((5, C, N))]
-        dzm, dx0, dpg0, dwp1, dwo0, vec2, vec3 = call(
+        wp = lambda k: ln_s(k) + proj_s(k) + [pick(k, C, 640)] + bp_s(k)
+        dzm, dx0, dpg0, dwp1, dwo0, vec2, vec3, dx0k = call(
             midb_kernel, 4,
             [cm_spec(same), cm_spec(same), rows_spec((C, N), own), rows_spec((C, N), own), rows_spec((N,), own),
-             rows_spec((C, N), same), rows_spec((C, N), same), cm_spec(own), rows_spec((C, N), own)] + wp + smb,
-            [rows_spec((C, N), same), cm_spec(same), rows_spec((C, N), same), full((640, C)), full((C, C)), full((6, C, N)), full((4, C, N))],
-            [rt_own, sds((C, 64, N), BF16), rt_own, sds((640, C), F32), sds((C, C), F32), sds((6, C, N), F32), sds((4, C, N), F32)],
-            [scr(), scr(), scr(), scr(), pltpu.VMEM((640, N), BF16)], "midb")(
-            da1, db1, zh1, zm, mask_all, dpg1, dzt, x0, zh0, lni[1], wt[1], w_proj[1], bp[1],
-            lnm[0], wot[0], w_out[0], bo[0], wt[0, 512:], bp[0, 4])
-        dx0c = lax.all_to_all(dx0, "dap", 2, 1, axis_index_groups=QUAD, tiled=True)
+             rows_spec((C, N), same), rows_spec((C, N), same), cm_spec(own), rows_spec((C, N), own)] + wp(1) + smb(0),
+            [rows_spec((C, N), same), cm_spec(same), rows_spec((C, N), same), full((640, C)), full((C, C)), full((6, C, C)), full((4, C, C)), ANY],
+            [rt_own, sds((C, 64, N), BF16), rt_own, sds((640, C), F32), sds((C, C), F32), sds((6, C, C), F32), sds((4, C, C), F32), sds((C, N, 128), BF16)],
+            [scr(), scr(), scr(), scr(), pltpu.VMEM((640, GR * N), BF16), scr(), pltpu.VMEM((2, C, RB, N), BF16)]
+            + [pltpu.SemaphoreType.DMA((k,)) for k in (2, 2, 4, 2, 4, 4, 4)], "midb", 4)(
+            da1, db1, zh1, zm, mask_all, dpg1, dzt, x0, g0, prm, wt, w_proj, prm,
+            prm, wot, w_out, prm)
         da0 = jnp.einsum("cij,cjk->cik", dx0, b0f, preferred_element_type=F32).astype(BF16)
-        db0 = jnp.einsum("cij,cik->cjk", dx0c, a0f, preferred_element_type=F32).astype(BF16)
-
-        dzp, dwp0, vec4 = call(
+        db0 = jnp.einsum("cij,cik->cjk", dx0k, a0f, preferred_element_type=F32).astype(BF16)
+
+        dzp, zo, dwp0, vec4 = call(
             last_kernel, 4,
-            [cm_spec(same), cm_spec(same), rows_spec((C, N), own), rows_spec((C, N), own), rows_spec((N,), own),
-             rows_spec((C, N), same), rows_spec((C, N), same)] + wp,
-            [rows_spec((N, C), same), full((640, C)), full((6, C, N))],
-            [sds((64, N, C), BF16), sds((640, C), F32), sds((6, C, N), F32)],
-            [scr(), scr(), pltpu.VMEM((640, N), BF16)], "last")(
-            da0, db0, zh0, zt0, mask_all, dpg0, dzm, lni[0], wt[0], w_proj[0], bp[0])
+            [cm_spec(same), cm_spec(lambda i: i + 4 * partner(0)[0]), rows_spec((C, N), own), rows_spec((C, N), own), rows_spec((N,), own),
+             rows_spec((C, N), same), rows_spec((C, N), same), rows_spec((C, N), same)] + wp(0),
+            [rows_spec((N, C), same), rows_spec((N, C), same), full((640, C)), full((6, C, C))],
+            [sds((64, N, C), BF16), sds((64, N, C), BF16), sds((640, C), F32), sds((6, C, C), F32)],
+            [scr(), scr(), pltpu.VMEM((640, GR * N), BF16)], "last")(
+            da0, db0, zh0, zt0, mask_all, dpg0, dzm, zo, prm, wt, w_proj, prm)
 
         g = reduce_all(dwp0, dwo0, vec4, vec3, dwp1, dwo1, vec2, vec1)[:1568].reshape(2, 784, C)
         d_b = jnp.concatenate([g[:, 768:772].reshape(2, 512), g[:, 777]], axis=1)

time: 506 us -> 433 us (0.86)
  local copies, waits for them, and re-layouts: 46 us -> 11.1 us
  waiting for transfers between devices: 35.8 us -> 9.71 us
  Pallas kernels: 330 us -> 323 us
    all_to_all x1 -> x0, waiting for transfers between devices: 35.8 us -> none  [local_step(): dx0c = lax.all_to_all(dx0, 'dap', 2, 1, axis_index_groups=QUAD, tiled=True)]
    all_to_all x2 -> x0, local copies, waits for them, and re-layouts: 14.2 us -> none  [local_step(): dx0c = lax.all_to_all(dx0, 'dap', 2, 1, axis_index_groups=QUAD, tiled=True)]
    pallas_call x1, Pallas kernels: 64.4 us -> 51.3 us  [local_step(): call(mid_kernel, 8, [cm_spec(rb), rows_spec((C, N), rb), rows_spec((C, N)...]
    pallas_call x1, Pallas kernels: 55.6 us -> 66.9 us  [local_step(): call(midb_kernel, 4, [cm_spec(same), cm_spec(same), rows_spec((C, N), own...]
    ppermute x1, waiting for transfers between devices: 0.01 us -> 9.71 us  [local_step(): dz_oth = lax.ppermute(dz_own, 'dap', SWAP_X)]
    pallas_call x1, Pallas kernels: 40.9 us -> 33.2 us  [local_step(): call(post1_kernel, 8, [cm_spec(rb), rows_spec((C, N), rb), rows_spec((C,...]
    pallas_call x1 -> x0, local copies, waits for them, and re-layouts: 7.32 us -> none  [local_step(): call(midb_kernel, 4, [cm_spec(same), cm_spec(same), rows_spec((C, N), own...]
    broadcast_in_dim x14 -> x1, local copies, waits for them, and re-layouts: 8.22 us -> 1.92 us  [local_step(): prm = jnp.broadcast_to(prm[..., None], (2, 10, C, N))]
  transfers between devices with their start and end apart: 2 -> 1, of which waited for: 1 -> 1; matrix products, arithmetic and copies ran while one was open for 10% -> 7% of each run, Pallas kernels for 13% -> 12%
where the time goes in v2:
time: 433 us
  Pallas kernels  323 us (75%)
  matrix products  84.5 us (20%)
  local copies, waits for them, and re-layouts  11.1 us (3%)
  waiting for transfers between devices  9.71 us (2%)
    pallas_call x1, Pallas kernels, local_step(): call(pre_kernel, 8, [ANY, vm] + ln_s(0) + proj_s(0) + bp_s(0), [cm_spec(r...  107 us
    pallas_call x1, Pallas kernels, local_step(): call(midb_kernel, 4, [cm_spec(same), cm_spec(same), rows_spec((C, N), own...  66.9 us
    pallas_call x1, Pallas kernels, local_step(): call(mid_kernel, 8, [cm_spec(rb), rows_spec((C, N), rb), rows_spec((C, N)...  51.3 us
    pallas_call x1, Pallas kernels, local_step(): call(last_kernel, 4, [cm_spec(same), cm_spec(lambda i: i + 4 * partner(0)...  38 us
    pallas_call x1, Pallas kernels, local_step(): call(post1_kernel, 8, [cm_spec(rb), rows_spec((C, N), rb), rows_spec((C,...  33.2 us
    pallas_call x1, Pallas kernels, reduce_all(): pl.pallas_call(reduce_kernel, name='reduce', out_shape=sds((GROWS, C), F3...  27.1 us
    dot_general x1, matrix products, local_step(): jnp.einsum('ckj,cij->cki', b1o, dx1f, preferred_element_type=F32)  17 us
    dot_general x1, matrix products, local_step(): x1 = jnp.einsum('cki,ckj->cij', a1c, b1f, preferred_element_type=F32)  15.6 us
  transfers between devices with their start and end apart: 1, of which 1 were waited for; matrix products, arithmetic and copies ran while one was open for 7% of the time, Pallas kernels for 12%

profile of v2, /device:TPU:0, one launch (start us, length us, event | category | flops | bytes accessed | tf_op | source)
XLA Modules:
  0.0 432.7 jit_solution(7288206638100140486)
XLA Ops:
  0.6 0.7 copy.33
  1.3 0.7 concatenate.15
  2.0 0.8 convert_element_type.28
  3.1 0.8 convert_element_type.31.m_ref
  3.9 1.9 copy.34
  5.8 0.7 maximum_convert_fusion
  6.5 1.9 broadcast_in_dim.6.ln_ref.bp_ref.lnm_ref.bo_ref
  8.4 106.9 %pre.1 = (bf16[128,128,256]{2,1,0:T(8,128)(2,1)}, bf16[128,128,256]{2,1,0:T(8,128)(2,1)}, bf16[128,128,256]{2,1,0:T(8,128)(2,1)}, f32[128,128,256]{2,1,0:T(8,128...) custom-call(bf16[64,256,128]{2,1,0:T(8,128)(2,1)} %bitcast.38, ...), custom_call_target="tpu_custom_call" | custom-call | tf_op jit(solution)/shard_map/pre/pallas_call | solution.py:596
  115.3 1.1 collective-permute-start
  116.4 0.7 copy.35
  117.1 14.3 %fusion.2.x_ref.x0_ref = f32[128,128,256]{2,1,0:T(8,128)} fusion(bf16[128,128,256]{2,1,0:T(8,128)(2,1)} %get-tuple-element.43, bf16[128,256,256]{2,1,0:T(8,128)(2,1)} %get-tuple-element.44), kind=kOutput, calls=%fused_computation.12 | convolution fusion | flops 2147483648 | bytes 41943040 | tf_op jit(solution)/shard_map/cik,cjk->cij/dot_general | solution.py:604
  131.4 51.3 %mid.1 = (bf16[128,128,256]{2,1,0:T(8,128)(2,1)}, bf16[128,128,256]{2,1,0:T(8,128)(2,1)}, f32[128,128,256]{2,1,0:T(8,128)}, bf16[128,64,256]{2,1,0:T(8,128)(2,1)...) custom-call(f32[128,128,256]{2,1,0:T(8,128)} %fusion.2.x_ref.x0_ref, ...), custom_call_target="tpu_custom_call" | custom-call | tf_op jit(solution)/shard_map/mid/pallas_call | solution.py:606
  182.7 15.6 %fusion.3.x_ref = f32[128,128,256]{2,1,0:T(8,128)} fusion(bf16[128,256,128]{2,1,0:T(8,128)(2,1)} %get-tuple-element.49, bf16[128,256,256]{2,1,0:T(8,128)(2,1)} %get-tuple-element.50), kind=kOutput, calls=%fused_computation.13 | convolution fusion | flops 2147483648 | bytes 41943040 | tf_op jit(solution)/shard_map/cki,ckj->cij/dot_general | solution.py:613
  198.4 9.7 %collective-permute-done.dzo_ref = bf16[64,256,128]{2,1,0:T(8,128)(2,1)} collective-permute-done((bf16[64,256,128]{2,1,0:T(8,128)(2,1)}, bf16[64,256,128]{2,1,0:T(8,128)(2,1)}, u32[]{:S(2)}, u32[]{:S(2)}) %collective-permute-start) | collective-permute-done | bytes 4194336 | tf_op jit(solution)/shard_map/ppermute | solution.py:603
  208.1 33.2 %post1.1 = (bf16[64,128,256]{2,1,0:T(8,128)(2,1)}, bf16[64,128,256]{2,1,0:T(8,128)(2,1)}, bf16[64,128,256]{2,1,0:T(8,128)(2,1)}, f32[128,128]{1,0:T(8,128)}, f32...) custom-call(f32[128,128,256]{2,1,0:T(8,128)} %fusion.3.x_ref, f32[128,128,256]{2,1,0:T(8,128)} %get-tuple-element.51.g_ref, ...), custom_call_target="tpu_custom_call" | custom-call | tf_op jit(solution)/shard_map/post1/pallas_call | solution.py:617
  241.3 12.2 %convolution_convert_fusion.2.db_ref = bf16[128,64,256]{2,1,0:T(8,128)(2,1)} fusion(bf16[128,64,256]{2,1,0:T(8,128)(2,1)} %get-tuple-element.55, bf16[128,256,256]{2,1,0:T(8,128)(2,1)} %get-tuple-element.54), kind=kOutput, calls=%fused_computation.2 | convolution fusion | flops 1075838976 | bytes 25165824 | tf_op jit(solution)/shard_map/cki,cij->ckj/dot_general | solution.py:625
  253.5 17.0 %convolution_convert_fusion.3.da_ref = bf16[128,64,256]{2,1,0:T(8,128)(2,1)} fusion(bf16[128,64,256]{2,1,0:T(8,128)(2,1)S(1)} %copy-done, bf16[128,256,256]{2,1,0:T(8,128)(2,1)} %get-tuple-element.54), kind=kOutput, calls=%fused_computation.3 | convolution fusion | flops 1075838976 | bytes 25165824 | tf_op jit(solution)/shard_map/ckj,cij->cki/dot_general | solution.py:624
  270.6 66.9 %midb.1 = (bf16[64,128,256]{2,1,0:T(8,128)(2,1)}, bf16[128,64,256]{2,1,0:T(8,128)(2,1)}, bf16[64,128,256]{2,1,0:T(8,128)(2,1)}, f32[640,128]{1,0:T(8,128)}, f32[...) custom-call(bf16[128,64,256]{2,1,0:T(8,128)(2,1)} %convolution_convert_fusion., ...), custom_call_target="tpu_custom_call" | custom-call | tf_op jit(solution)/shard_map/midb/pallas_call | solution.py:629
  337.5 12.0 %convolution_convert_fusion.1.da_ref = bf16[128,64,256]{2,1,0:T(8,128)(2,1)} fusion(bf16[128,64,256]{2,1,0:T(8,128)(2,1)} %get-tuple-element.59, bf16[128,256,256]{2,1,0:T(8,128)(2,1)} %get-tuple-element.44), kind=kOutput, calls=%fused_computation.1 | convolution fusion | flops 1075838976 | bytes 25165824 | tf_op jit(solution)/shard_map/cij,cjk->cik/dot_general | solution.py:639
  349.5 13.3 %convolution_convert_fusion.db_ref = bf16[128,128,256]{2,1,0:T(8,128)(2,1)} fusion(bf16[128,256,128]{2,1,0:T(8,128)(2,1)} %get-tuple-element.60, bf16[128,256,256]{2,1,0:T(8,128)(2,1)} %get-tuple-element.61), kind=kOutput, calls=%fused_computation | convolution fusion | flops 2151677952 | bytes 33554432 | tf_op jit(solution)/shard_map/cij,cik->cjk/dot_general | solution.py:640
  362.8 38.0 %last.1 = (bf16[64,256,128]{2,1,0:T(8,128)(2,1)}, bf16[64,256,128]{2,1,0:T(8,128)(2,1)}, f32[640,128]{1,0:T(8,128)}, f32[6,128,128]{2,1,0:T(8,128)}) custom-call(bf16[128,64,256]{2,1,0:T(8,128)(2,1)} %convolution_convert_fusion.1.da_ref, bf16[128,128,256]{2,1,0:T(8,128)(2,1)} %convolution_convert_fusion.db_ref, ...), custom_call_target="tpu_custom_call" | custom-call | tf_op jit(solution)/shard_map/last/pallas_call | solution.py:642
  400.8 27.1 %reduce.1 = f32[1664,128]{1,0:T(8,128)} custom-call(f32[640,128]{1,0:T(8,128)} %get-tuple-element.68.dwp0_ref, f32[128,128]{1,0:T(8,128)} %get-tuple-element.69.dwo0_ref, f32[6,128,128]{2,1,0:T(8,128)} %get-tuple-element.70.pre0_ref, f32[4,128,128]{2,1,0:T(8,128)} %get-tuple-element.71.post0_ref, f32[640,128]{1,0:T(8,128)} %get-tuple-element.72.dwp1_ref, ...), custom_call_target="tpu_custom_call" | custom-call | tf_op jit(solution)/shard_map/reduce/pallas_call | solution.py:550
  427.9 1.2 slice.24
  431.0 1.1 copy.39
  (13 shorter events, 2.7 us)
Async XLA Ops:
  0.6 115.7 %copy-start.1 = (bf16[2,128,128]{2,1,0:T(8,128)(2,1)S(1)}, bf16[2,128,128]{2,1,0:T(8,128)(2,1)}, u32[]{:S(2)}) copy-start(bf16[2,128,128]{2,1,0:T(8,128)(2,1)} %wo_ref.3) | copy-start | bytes 196612
  115.3 92.8 %collective-permute-start = (bf16[64,256,128]{2,1,0:T(8,128)(2,1)}, bf16[64,256,128]{2,1,0:T(8,128)(2,1)}, u32[]{:S(2)}, u32[]{:S(2)}) collective-permute-start(bf16[64,256,128]{2,1,0:T(8,128)(2,1)} %bitcast.39), channel_id=1, source_target_pairs={{0,2},{2,0},{1,3},{3,1},{4,6},{6,4},{5,7},{7,5},{8,10},{10,8},{9,1... | collective-permute-start | bytes 12582920 | tf_op jit(solution)/shard_map/ppermute | solution.py:603
  241.3 12.2 %copy-start = (bf16[128,64,256]{2,1,0:T(8,128)(2,1)S(1)}, bf16[128,64,256]{2,1,0:T(8,128)(2,1)}, u32[]{:S(2)}) copy-start(bf16[128,64,256]{2,1,0:T(8,128)(2,1)} %get-tuple-element.48) | copy-start | bytes 12582916

commit v3 on v2

--- a/solution.py
+++ b/solution.py
@@ -9,12 +9,16 @@
 LN_EPS = 1e-5
 RB = 16
 SP = 17
-UN = 8
-GR = 4
+UN = 16
+GR = 8
+CB = 16
+DZ1 = 48
 F32 = jnp.float32
 BF16 = jnp.bfloat16
 C = 128
 N = 256
+HB = 64
+CP = 640
 SWAP_X = [(0, 2), (2, 0), (1, 3), (3, 1)]
 
 
@@ -45,7 +49,7 @@
 
 
 def perm_cols(t):
-    return jnp.concatenate([t[0:64], t[128:192], t[64:128], t[192:256]], axis=0)
+    return jnp.concatenate([t[0:HB], t[C:192], t[HB:C], t[192:N]], axis=0)
 
 
 def load_t(ref, r):
@@ -57,14 +61,14 @@
 
 
 def by_chip(v):
-    v0, v1 = v[:, :128], v[:, 128:]
-    low = lax.broadcasted_iota(jnp.int32, (C, 128), 1) < 64
-    return jnp.concatenate([jnp.where(low, v0, pltpu.roll(v1, 64, 1)), jnp.where(low, pltpu.roll(v0, 64, 1), v1)], axis=1)
+    v0, v1 = v[:, :C], v[:, C:]
+    low = lax.broadcasted_iota(jnp.int32, (C, C), 1) < HB
+    return jnp.concatenate([jnp.where(low, v0, pltpu.roll(v1, HB, 1)), jnp.where(low, pltpu.roll(v0, HB, 1), v1)], axis=1)
 
 
 def put_row(scr, r, val):
     for h in range(2):
-        scr[h, pl.ds(r, C, stride=SP), :] = val[:, h * 128:(h + 1) * 128]
+        scr[h, pl.ds(r, C, stride=SP), :] = val[:, h * C:(h + 1) * C]
 
 
 def get_row(scr, r):
@@ -76,7 +80,7 @@
         c0 = i * 8
         for k in range(8):
             for h in range(2):
-                out_ref[c0 + k, :, h * 128:(h + 1) * 128] = scr[h, pl.ds((c0 + k) * SP, RB), :].astype(out_ref.dtype)
+                out_ref[c0 + k, :, h * C:(h + 1) * C] = scr[h, pl.ds((c0 + k) * SP, RB), :].astype(out_ref.dtype)
         return 0
     lax.fori_loop(0, C // 8, body, 0)
 
@@ -86,16 +90,16 @@
         c0 = i * 8
         for k in range(8):
             for h in range(2):
-                scr[h, pl.ds((c0 + k) * SP, RB), :] = in_ref[c0 + k, :, h * 128:(h + 1) * 128].astype(F32)
+                scr[h, pl.ds((c0 + k) * SP, RB), :] = in_ref[c0 + k, :, h * C:(h + 1) * C].astype(F32)
         return 0
     lax.fori_loop(0, C // 8, body, 0)
 
 
 def gates(zh, m, wt, bp, scr_a, scr_b, g_ref, r):
     p = dot(wt[...], zh)
-    put_row(scr_a, r, sig(p[0:128] + bp[0]) * (p[128:256] + bp[1]) * m)
-    put_row(scr_b, r, sig(p[256:384] + bp[2]) * (p[384:512] + bp[3]) * m)
-    g_ref[r] = sig(p[512:640] + bp[4])
+    put_row(scr_a, r, sig(p[0:C] + bp[0]) * (p[C:N] + bp[1]) * m)
+    put_row(scr_b, r, sig(p[N:384] + bp[2]) * (p[384:512] + bp[3]) * m)
+    g_ref[r] = sig(p[512:CP] + bp[4])
 
 
 def groups(body):
@@ -103,10 +107,10 @@
 
 
 def halves(v):
-    return v[:, :128] + v[:, 128:]
-
-
-CHUNKS = ((0, 640, (0, 1, 2, 3)), (640, 512, (0, 2, 3, 1)), (1152, 512, (0, 3, 1, 2)))
+    return v[:, :C] + v[:, C:]
+
+
+CHUNKS = ((0, CP, (0, 1, 2, 3)), (CP, 512, (0, 2, 3, 1)), (1152, 512, (0, 3, 1, 2)))
 GROWS = 1664
 
 
@@ -145,11 +149,11 @@
 def pair_parts(step, st, out, split):
     bit = partner(0)[0]
     slot = lax.rem(step, 2)
-    dst = out.at[:, pl.ds(pl.multiple_of(bit * 128 + rb(step) * RB, RB), RB), :]
+    dst = out.at[:, pl.ds(pl.multiple_of(bit * C + rb(step) * RB, RB), RB), :]
     mine = theirs = st.at[slot]
     if split:
-        mine = st.at[slot, :, :, pl.ds(pl.multiple_of(bit * 128, 128), 128)]
-        theirs = st.at[slot, :, :, pl.ds(pl.multiple_of((1 - bit) * 128, 128), 128)]
+        mine = st.at[slot, :, :, pl.ds(pl.multiple_of(bit * C, C), C)]
+        theirs = st.at[slot, :, :, pl.ds(pl.multiple_of((1 - bit) * C, C), C)]
     return slot, dst, mine, theirs
 
 
@@ -188,8 +192,8 @@
     return [pltpu.VMEM((2, C, RB, N), BF16), pltpu.SemaphoreType.DMA((2,)), pltpu.SemaphoreType.DMA((2,)), pltpu.SemaphoreType.DMA((8,))]
 
 
-def pre_kernel(z_ref, m_ref, ln_ref, wt_ref, bp_ref, a_ref, zh_ref, zt_ref, g_ref, mall_ref, af_ref, bf_ref,
-               scr_a, scr_b, mbuf, zbuf, zloc, zsend, zrecv, msem, st_a, la, sa, ra, st_b, lb, sb, rb_):
+def pre_kernel(z_ref, dz_ref, m_ref, ln_ref, wt_ref, bp_ref, a_ref, zh_ref, zt_ref, g_ref, mall_ref, af_ref, bf_ref, dzs_ref,
+               scr_a, scr_b, dzbuf, dzsem, mbuf, zbuf, zloc, zsend, zrecv, msem, st_a, la, sa, ra, st_b, lb, sb, rb_):
     step = pl.program_id(0)
     xb = partner(1)[0]
 
@@ -197,9 +201,28 @@
         return pltpu.make_async_copy(z_ref.at[pl.ds(q * RB, RB)], zbuf.at[pl.ds(q * RB, RB)], zloc.at[q])
 
     def z_there(q):
-        return remote(z_ref.at[pl.ds(q * RB, RB)], zbuf.at[pl.ds(64 + q * RB, RB)], zsend.at[q], zrecv.at[q], 1)
-
-    m_dst = mbuf.at[pl.ds(pl.multiple_of(xb * 64, 64), 64), :]
+        return remote(z_ref.at[pl.ds(q * RB, RB)], zbuf.at[pl.ds(HB + q * RB, RB)], zsend.at[q], zrecv.at[q], 1)
+
+    def dz_in():
+        return pltpu.make_async_copy(dz_ref.at[pl.ds(0, DZ1)], dzbuf, dzsem.at[0])
+
+    def dz_out():
+        return pltpu.make_async_copy(dzbuf, dzs_ref, dzsem.at[1])
+
+    @pl.when(step == 1)
+    def _():
+        dz_in().start()
+
+    @pl.when(step == 3)
+    def _():
+        dz_in().wait()
+        dz_out().start()
+
+    @pl.when(step == 6)
+    def _():
+        dz_out().wait()
+
+    m_dst = mbuf.at[pl.ds(pl.multiple_of(xb * HB, HB), HB), :]
 
     def m_there():
         return remote(m_ref, m_dst, msem.at[1], msem.at[2], 1)
@@ -298,20 +321,35 @@
         ref[...] = jnp.zeros_like(ref)
 
 
-def post1_kernel(x_ref, g_ref, zm_ref, dz_ref, dzo_ref, lnm_ref, wot_ref, wo_ref, bo_ref,
-                 zo_ref, dpg_ref, dzt_ref, dwo_ref, vec_ref, dxf_ref, scr_x, scr_d, st, lsem, ssem, rsem):
+def post1_kernel(x_ref, g_ref, zm_ref, dz_ref, dzo_ref, dzall_ref, lnm_ref, wot_ref, wo_ref, bo_ref,
+                 zo_ref, dpg_ref, dzt_ref, dwo_ref, vec_ref, dxf_ref, scr_x, scr_d, dzbuf, dzsem, st, lsem, ssem, rsem):
     step = pl.program_id(0)
 
+    def dz_there():
+        return remote(dzall_ref.at[pl.ds(DZ1, RB)], dzbuf.at[1], dzsem.at[0], dzsem.at[1], 1)
+
     @pl.when(step == 0)
     def _():
-        greet((0,))
+        greet((0, 1))
+        dz_there().start()
         zero(dwo_ref, vec_ref)
     unpack(x_ref, scr_x)
 
+    @pl.when((step >= 4) & (step < 7))
+    def _():
+        def copy_row(r, _):
+            dzbuf[0, r] = dzo_ref[r]
+            return 0
+        lax.fori_loop(0, RB, copy_row, 0)
+
+    @pl.when(step == 7)
+    def _():
+        dz_there().wait()
+
     @pl.when(step >= 4)
     def _():
         def row(r, _):
-            dz = load_t(dzo_ref, r)
+            dz = load_t(dzbuf.at[step // 7], r)
             res = post_row(get_row(scr_x, r), g_ref[r], lnm_ref, wot_ref, wo_ref, bo_ref, dz)
             put_row(scr_d, r, res[-1])
             return 0
@@ -343,16 +381,16 @@
     p = dot(wt_ref[0:512, :], zh)
     cols = slice(k * N, k * N + N)
     for q, scr in ((0, scr_a), (1, scr_b)):
-        s = sig(p[q * 256:q * 256 + 128] + bp_ref[2 * q])
-        v = p[q * 256 + 128:q * 256 + 256] + bp_ref[2 * q + 1]
+        s = sig(p[q * N:q * N + C] + bp_ref[2 * q])
+        v = p[q * N + C:q * N + N] + bp_ref[2 * q + 1]
         d_s = get_row(scr, r) * m
         d_v = d_s * s
         d_g = d_v * v * (1.0 - s)
-        dp_ref[q * 256:q * 256 + 128, cols] = d_g.astype(BF16)
-        dp_ref[q * 256 + 128:q * 256 + 256, cols] = d_v.astype(BF16)
+        dp_ref[q * N:q * N + C, cols] = d_g.astype(BF16)
+        dp_ref[q * N + C:q * N + N, cols] = d_v.astype(BF16)
         vec_ref[2 * q] += halves(d_g)
         vec_ref[2 * q + 1] += halves(d_v)
-    dp_ref[512:640, cols] = d_pg
+    dp_ref[512:CP, cols] = d_pg
     d_zh = dot(w_ref[...], dp_ref[:, cols])
     zn, rstd = norm(z)
     vec_ref[4] += halves(d_zh * zn)
@@ -369,10 +407,10 @@
     xbit = partner(1)[0]
 
     def block(core, chip, k):
-        return dxk_ref.at[:, pl.ds(pl.multiple_of(core * 128 + chip * 64 + k * RB, RB), RB), :]
+        return dxk_ref.at[:, pl.ds(pl.multiple_of(core * C + chip * HB + k * RB, RB), RB), :]
 
     def part(k, chip):
-        return st.at[lax.rem(k, 2), :, :, pl.ds(pl.multiple_of(chip * 128, 128), 128)]
+        return st.at[lax.rem(k, 2), :, :, pl.ds(pl.multiple_of(chip * C, C), C)]
 
     def here(k):
         return pltpu.make_async_copy(part(k, xbit), block(cbit, xbit, k), lsem.at[lax.rem(k, 2)])
@@ -470,6 +508,22 @@
     groups(group)
 
 
+def grads1_kernel(a_ref, b_ref, dx_ref, da_ref, db_ref):
+    for k in range(CB):
+        dx = dx_ref[k]
+        da_ref[k] = dot(b_ref[k], jnp.transpose(dx)).astype(BF16)
+        db_ref[k] = dot(a_ref[k], dx).astype(BF16)
+
+
+def grads0_kernel(dx_ref, b_ref, dxk_ref, a_ref, da_ref, db_ref, turned):
+    own = pl.ds(pl.multiple_of(partner(0)[0] * HB, HB), HB)
+    for k in range(CB):
+        turned[k] = jnp.transpose(dxk_ref[k])
+        da_ref[k] = dot(dx_ref[k], b_ref[k]).astype(BF16)
+    for k in range(CB):
+        db_ref[k] = dot(turned[k, own, :], a_ref[k]).astype(BF16)
+
+
 def sds(shape, dtype):
     return jax.ShapeDtypeStruct(shape, dtype)
 
@@ -488,7 +542,7 @@
 
 
 def scr():
-    return pltpu.VMEM((2, C * SP, 128), F32)
+    return pltpu.VMEM((2, C * SP, C), F32)
 
 
 ANY = pl.BlockSpec(memory_space=pl.ANY)
@@ -504,8 +558,8 @@
     greet((0, 1, 2, 3))
     parts = ((dwp0_ref, dwo0_ref, pre0_ref, post0_ref), (dwp1_ref, dwo1_ref, pre1_ref, post1_ref))
     for k, (dwp, dwo, vpre, vpost) in enumerate(parts):
-        acc[784 * k:784 * k + 640, :] = dwp[...]
-        acc[784 * k + 640:784 * k + 768, :] = dwo[...]
+        acc[784 * k:784 * k + CP, :] = dwp[...]
+        acc[784 * k + CP:784 * k + 768, :] = dwo[...]
         rows = [jnp.sum(jnp.transpose(v[q]), axis=0, keepdims=True) for v, n in ((vpre, 6), (vpost, 4)) for q in range(n)]
         acc[784 * k + 768:784 * k + 784, :] = jnp.concatenate(rows + [jnp.zeros((6, C), F32)], axis=0)
     acc[1568:GROWS, :] = jnp.zeros((GROWS - 1568, C), F32)
@@ -556,7 +610,7 @@
 
 def solution(mesh):
     def local_step(z_pair, pair_mask, dz_out, ln_in, w_proj, b_proj, ln_mid, w_out, b_out):
-        mask = pair_mask[0].reshape(64, 2, 2, 64).transpose(0, 2, 1, 3).reshape(64, N).astype(F32)
+        mask = pair_mask[0].reshape(HB, 2, 2, HB).transpose(0, 2, 1, 3).reshape(HB, N).astype(F32)
 
         prm = jnp.concatenate([ln_in, ln_mid, b_out[:, None], b_proj.reshape(2, 5, C)], axis=1).astype(F32)
         prm = jnp.broadcast_to(prm[..., None], (2, 10, C, N))
@@ -579,78 +633,78 @@
             return [pl.BlockSpec((None, None, C, N), lambda i: (k, 4, 0, 0))]
 
         def proj_s(k):
-            return [pick(k, 640, C)]
+            return [pick(k, CP, C)]
 
         def bp_s(k):
             return [vecs(k, 5, 1)]
 
         same = lambda i: i
-        cm_all = sds((C, 128, N), BF16)
+        cm_all = sds((C, C, N), BF16)
         cm_full = sds((C, N, N), BF16)
-        cm_own = sds((C, 64, N), BF16)
-        rt_all = sds((128, C, N), BF16)
-        rt_f32 = sds((128, C, N), F32)
-        rt_own = sds((64, C, N), BF16)
+        cm_own = sds((C, HB, N), BF16)
+        rt_all = sds((C, C, N), BF16)
+        rt_f32 = sds((C, C, N), F32)
+        rt_own = sds((HB, C, N), BF16)
         vm = pl.BlockSpec(memory_space=pltpu.VMEM)
 
-        a0, zh0, zt0, g0, mask_all, a0f, b0f = call(
-            pre_kernel, 8, [ANY, vm] + ln_s(0) + proj_s(0) + bp_s(0),
-            [cm_spec(rb), rows_spec((C, N), rb), rows_spec((C, N), rb), rows_spec((C, N), rb), vm, ANY, ANY],
-            [cm_all, rt_all, rt_all, rt_f32, sds((128, N), F32), cm_full, cm_full],
-            [scr(), scr(), pltpu.VMEM((128, N), F32), pltpu.VMEM((128, N, C), BF16)] + [pltpu.SemaphoreType.DMA((4,))] * 3 + [pltpu.SemaphoreType.DMA((3,))] + ship_scratch() * 2,
-            "pre", 1)(z_pair[0], mask, prm, wt, prm)
-        dz_own, a0 = lax.optimization_barrier((dz_out[0], a0))
-        dz_oth = lax.ppermute(dz_own, "dap", SWAP_X)
+        a0, zh0, zt0, g0, mask_all, a0f, b0f, dz_head = call(
+            pre_kernel, 8, [ANY, ANY, vm] + ln_s(0) + proj_s(0) + bp_s(0),
+            [cm_spec(rb), rows_spec((C, N), rb), rows_spec((C, N), rb), rows_spec((C, N), rb), vm, ANY, ANY, ANY],
+            [cm_all, rt_all, rt_all, rt_f32, sds((C, N), F32), cm_full, cm_full, sds((DZ1, N, C), BF16)],
+            [scr(), scr(), pltpu.VMEM((DZ1, N, C), BF16), pltpu.SemaphoreType.DMA((2,)), pltpu.VMEM((C, N), F32), pltpu.VMEM((C, N, C), BF16)] + [pltpu.SemaphoreType.DMA((4,))] * 3 + [pltpu.SemaphoreType.DMA((3,))] + ship_scratch() * 2,
+            "pre", 1)(z_pair[0], dz_out[0], mask, prm, wt, prm)
+        dz_own = dz_out[0]
+        dz_oth = lax.ppermute(dz_head, "dap", SWAP_X)
         x0 = jnp.einsum("cik,cjk->cij", a0, b0f, preferred_element_type=F32)
 
         zm, zh1, g1, a1o, b1o, a1c, b1f = call(
             mid_kernel, 8,
             [cm_spec(rb), rows_spec((C, N), rb), rows_spec((C, N), rb), rows_spec((N,), rb)] + mid_s(0) + [pick(0, C, C)] + bias_s(0) + ln_s(1) + proj_s(1) + bp_s(1),
             [rows_spec((C, N), rb), rows_spec((C, N), rb), rows_spec((C, N), rb), cm_spec(first4), cm_spec(first4), ANY, ANY],
-            [rt_all, rt_all, rt_f32, cm_own, cm_own, sds((C, N, 128), BF16), cm_full],
+            [rt_all, rt_all, rt_f32, cm_own, cm_own, sds((C, N, C), BF16), cm_full],
             [scr(), scr(), scr()] + ship_scratch() * 2,
             "mid", 2)(x0, g0, zt0, mask_all, prm, wot, prm, prm, wt, prm)
         x1 = jnp.einsum("cki,ckj->cij", a1c, b1f, preferred_element_type=F32)
 
-        late = lambda i: lax.max(i - 4, 0)
+        late = lambda i: lax.min(lax.max(i - 4, 0), 2)
         smb = lambda k: mid_s(k) + [pick(k, C, C), pick(k, C, C)] + bias_s(k)
         zo, dpg1, dzt, dwo1, vec1, dx1f = call(
             post1_kernel, 8,
-            [cm_spec(rb), rows_spec((C, N), rb), rows_spec((C, N), rb), rows_spec((N, C), first4), rows_spec((N, C), late)] + smb(1),
+            [cm_spec(rb), rows_spec((C, N), rb), rows_spec((C, N), rb), rows_spec((N, C), first4), rows_spec((N, C), late), ANY] + smb(1),
             [rows_spec((C, N), first4), rows_spec((C, N), first4), rows_spec((C, N), first4), full((C, C)), full((4, C, C)), ANY],
             [rt_own, rt_own, rt_own, sds((C, C), F32), sds((4, C, C), F32), cm_full],
-            [scr(), scr()] + ship_scratch(), "post1", 3)(
-            x1, g1, zm, dz_own, dz_oth, prm, wot, w_out, prm)
-        da1 = jnp.einsum("ckj,cij->cki", b1o, dx1f, preferred_element_type=F32).astype(BF16)
-        db1 = jnp.einsum("cki,cij->ckj", a1o, dx1f, preferred_element_type=F32).astype(BF16)
+            [scr(), scr(), pltpu.VMEM((2, RB, N, C), BF16), pltpu.SemaphoreType.DMA((2,))] + ship_scratch(), "post1", 3)(
+            x1, g1, zm, dz_own, dz_oth, dz_own, prm, wot, w_out, prm)
+        chan = lambda *sh: pl.BlockSpec((CB,) + sh, lambda i: (i, 0, 0))
+        da1, db1 = call(grads1_kernel, C // CB, [chan(HB, N), chan(HB, N), chan(N, N)], [chan(HB, N)] * 2, [cm_own] * 2, [], "grads1")(a1o, b1o, dx1f)
 
         own = lambda i: i + 4 * partner(1)[0]
-        wp = lambda k: ln_s(k) + proj_s(k) + [pick(k, C, 640)] + bp_s(k)
+        wp = lambda k: ln_s(k) + proj_s(k) + [pick(k, C, CP)] + bp_s(k)
         dzm, dx0, dpg0, dwp1, dwo0, vec2, vec3, dx0k = call(
             midb_kernel, 4,
             [cm_spec(same), cm_spec(same), rows_spec((C, N), own), rows_spec((C, N), own), rows_spec((N,), own),
              rows_spec((C, N), same), rows_spec((C, N), same), cm_spec(own), rows_spec((C, N), own)] + wp(1) + smb(0),
-            [rows_spec((C, N), same), cm_spec(same), rows_spec((C, N), same), full((640, C)), full((C, C)), full((6, C, C)), full((4, C, C)), ANY],
-            [rt_own, sds((C, 64, N), BF16), rt_own, sds((640, C), F32), sds((C, C), F32), sds((6, C, C), F32), sds((4, C, C), F32), sds((C, N, 128), BF16)],
-            [scr(), scr(), scr(), scr(), pltpu.VMEM((640, GR * N), BF16), scr(), pltpu.VMEM((2, C, RB, N), BF16)]
+            [rows_spec((C, N), same), cm_spec(same), rows_spec((C, N), same), full((CP, C)), full((C, C)), full((6, C, C)), full((4, C, C)), ANY],
+            [rt_own, sds((C, HB, N), BF16), rt_own, sds((CP, C), F32), sds((C, C), F32), sds((6, C, C), F32), sds((4, C, C), F32), sds((C, N, C), BF16)],
+            [scr(), scr(), scr(), scr(), pltpu.VMEM((CP, GR * N), BF16), scr(), pltpu.VMEM((2, C, RB, N), BF16)]
             + [pltpu.SemaphoreType.DMA((k,)) for k in (2, 2, 4, 2, 4, 4, 4)], "midb", 4)(
             da1, db1, zh1, zm, mask_all, dpg1, dzt, x0, g0, prm, wt, w_proj, prm,
             prm, wot, w_out, prm)
-        da0 = jnp.einsum("cij,cjk->cik", dx0, b0f, preferred_element_type=F32).astype(BF16)
-        db0 = jnp.einsum("cij,cik->cjk", dx0k, a0f, preferred_element_type=F32).astype(BF16)
+        da0, db0 = call(grads0_kernel, C // CB, [chan(HB, N), chan(N, N), chan(N, C), chan(N, N)], [chan(HB, N)] * 2, [cm_own] * 2,
+                        [pltpu.VMEM((CB, C, N), BF16)], "grads0")(dx0, b0f, dx0k, a0f)
 
         dzp, zo, dwp0, vec4 = call(
             last_kernel, 4,
-            [cm_spec(same), cm_spec(lambda i: i + 4 * partner(0)[0]), rows_spec((C, N), own), rows_spec((C, N), own), rows_spec((N,), own),
+            [cm_spec(same), cm_spec(same), rows_spec((C, N), own), rows_spec((C, N), own), rows_spec((N,), own),
              rows_spec((C, N), same), rows_spec((C, N), same), rows_spec((C, N), same)] + wp(0),
-            [rows_spec((N, C), same), rows_spec((N, C), same), full((640, C)), full((6, C, C))],
-            [sds((64, N, C), BF16), sds((64, N, C), BF16), sds((640, C), F32), sds((6, C, C), F32)],
-            [scr(), scr(), pltpu.VMEM((640, GR * N), BF16)], "last")(
+            [rows_spec((N, C), same), rows_spec((N, C), same), full((CP, C)), full((6, C, C))],
+            [sds((HB, N, C), BF16), sds((HB, N, C), BF16), sds((CP, C), F32), sds((6, C, C), F32)],
+            [scr(), scr(), pltpu.VMEM((CP, GR * N), BF16)], "last")(
             da0, db0, zh0, zt0, mask_all, dpg0, dzm, zo, prm, wt, w_proj, prm)
 
         g = reduce_all(dwp0, dwo0, vec4, vec3, dwp1, dwo1, vec2, vec1)[:1568].reshape(2, 784, C)
         d_b = jnp.concatenate([g[:, 768:772].reshape(2, 512), g[:, 777]], axis=1)
-        return (zo[None], dzp[None], g[:, 772:774], jnp.swapaxes(g[:, :640], 1, 2), d_b, g[:, 775:777], g[:, 640:768], g[:, 774])
+        return (zo[None], dzp[None], g[:, 772:774], jnp.swapaxes(g[:, :CP], 1, 2), d_b, g[:, 775:777], g[:, CP:768], g[:, 774])
 
     row_spec = P("dp", "dap")
     return jax.shard_map(local_step, mesh=mesh, in_specs=(row_spec, row_spec, row_spec, P(), P(), P(), P(), P(), P()), out_specs=(row_spec, row_spec, P(), P(), P(), P(), P(), P()), check_vma=False)

time: 433 us -> 404 us (0.933)
  matrix products: 84.5 us -> 29.9 us
  Pallas kernels: 323 us -> 358 us
  waiting for transfers between devices: 9.71 us -> 0.01 us
    dot_general x4 -> x0, matrix products: 54.5 us -> none  [the longest x1 17 us: local_step(): jnp.einsum('ckj,cij->cki', b1o, dx1f, preferred_element_type=F32)]
    pallas_call x2 -> x4, Pallas kernels: 145 us -> 179 us  [the longest x1 107 us: local_step(): call(pre_kernel, 8, [ANY, ANY, vm] + ln_s(0) + proj_s(0) + bp_s(0), [cm_s...]
    ppermute x1, waiting for transfers between devices: 9.71 us -> 0.01 us  [local_step(): dz_oth = lax.ppermute(dz_head, 'dap', SWAP_X)]
  transfers between devices with their start and end apart: 1 -> 1, of which waited for: 1 -> 0; matrix products, arithmetic and copies ran while one was open for 7% -> 8% of each run, Pallas kernels for 12% -> 12%
where the time goes in v3:
time: 404 us
  Pallas kernels  358 us (89%)
  matrix products  29.9 us (7%)
  local copies, waits for them, and re-layouts  12.6 us (3%)
    pallas_call x1, Pallas kernels, local_step(): call(pre_kernel, 8, [ANY, ANY, vm] + ln_s(0) + proj_s(0) + bp_s(0), [cm_s...  107 us
    pallas_call x1, Pallas kernels, local_step(): call(midb_kernel, 4, [cm_spec(same), cm_spec(same), rows_spec((C, N), own...  66.2 us
    pallas_call x1, Pallas kernels, local_step(): call(mid_kernel, 8, [cm_spec(rb), rows_spec((C, N), rb), rows_spec((C, N)...  49.8 us
    pallas_call x1, Pallas kernels, local_step(): call(last_kernel, 4, [cm_spec(same), cm_spec(same), rows_spec((C, N), own...  37.1 us
    pallas_call x1, Pallas kernels, local_step(): call(post1_kernel, 8, [cm_spec(rb), rows_spec((C, N), rb), rows_spec((C,...  34.7 us
    pallas_call x1, Pallas kernels, reduce_all(): pl.pallas_call(reduce_kernel, name='reduce', out_shape=sds((GROWS, C), F3...  27.4 us
    pallas_call x1, Pallas kernels, local_step(): call(grads0_kernel, C // CB, [chan(HB, N), chan(N, N), chan(N, C), chan(N...  19 us
    pallas_call x1, Pallas kernels, local_step(): call(grads1_kernel, C // CB, [chan(HB, N), chan(HB, N), chan(N, N)], [cha...  16.4 us
  transfers between devices with their start and end apart: 1, of which 0 were waited for; matrix products, arithmetic and copies ran while one was open for 8% of the time, Pallas kernels for 12%

profile of v3, /device:TPU:0, one launch (start us, length us, event | category | flops | bytes accessed | tf_op | source)
XLA Modules:
  0.0 404.1 jit_solution(4247025841127530445)
XLA Ops:
  0.6 0.7 copy.31
  1.3 0.7 concatenate.15
  2.0 0.8 convert_element_type.16
  3.0 0.8 convert_element_type.19.m_ref
  3.8 1.9 copy.32
  5.7 0.7 maximum_convert_fusion
  6.5 1.9 broadcast_in_dim.6.ln_ref.bp_ref.lnm_ref.bo_ref
  8.3 106.9 %pre.1 = (bf16[128,128,256]{2,1,0:T(8,128)(2,1)}, bf16[128,128,256]{2,1,0:T(8,128)(2,1)}, bf16[128,128,256]{2,1,0:T(8,128)(2,1)}, f32[128,128,256]{2,1,0:T(8,128...) custom-call(bf16[64,256,128]{2,1,0:T(8,128)(2,1)} %bitcast.33, ...), custom_call_target="tpu_custom_call" | custom-call | tf_op jit(solution)/shard_map/pre/pallas_call | solution.py:650
  115.2 1.1 collective-permute-start
  116.3 0.7 copy.33
  117.0 14.3 %fusion.2.x_ref.x0_ref = f32[128,128,256]{2,1,0:T(8,128)} fusion(bf16[128,128,256]{2,1,0:T(8,128)(2,1)} %get-tuple-element.45, bf16[128,256,256]{2,1,0:T(8,128)(2,1)} %get-tuple-element.46.b_ref), kind=kOutput, calls=%fused_computation.8 | convolution fusion | flops 2147483648 | bytes 41943040 | tf_op jit(solution)/shard_map/cik,cjk->cij/dot_general | solution.py:658
  131.3 49.8 %mid.1 = (bf16[128,128,256]{2,1,0:T(8,128)(2,1)}, bf16[128,128,256]{2,1,0:T(8,128)(2,1)}, f32[128,128,256]{2,1,0:T(8,128)}, bf16[128,64,256]{2,1,0:T(8,128)(2,1)...) custom-call(f32[128,128,256]{2,1,0:T(8,128)} %fusion.2.x_ref.x0_ref, ...), custom_call_target="tpu_custom_call" | custom-call | tf_op jit(solution)/shard_map/mid/pallas_call | solution.py:660
  181.1 15.6 %fusion.3.x_ref = f32[128,128,256]{2,1,0:T(8,128)} fusion(bf16[128,256,128]{2,1,0:T(8,128)(2,1)} %get-tuple-element.52, bf16[128,256,256]{2,1,0:T(8,128)(2,1)} %get-tuple-element.53), kind=kOutput, calls=%fused_computation.9 | convolution fusion | flops 2147483648 | bytes 41943040 | tf_op jit(solution)/shard_map/cki,ckj->cij/dot_general | solution.py:667
  196.8 1.7 copy-done
  198.4 34.7 %post1.1 = (bf16[64,128,256]{2,1,0:T(8,128)(2,1)}, bf16[64,128,256]{2,1,0:T(8,128)(2,1)}, bf16[64,128,256]{2,1,0:T(8,128)(2,1)}, f32[128,128]{1,0:T(8,128)}, f32...) custom-call(f32[128,128,256]{2,1,0:T(8,128)} %fusion.3.x_ref, f32[128,128,256]{2,1,0:T(8,128)} %get-tuple-element.54.g_ref, ...), custom_call_target="tpu_custom_call" | custom-call | tf_op jit(solution)/shard_map/post1/pallas_call | solution.py:671
  233.1 16.4 %grads1.1 = (bf16[128,64,256]{2,1,0:T(8,128)(2,1)}, bf16[128,64,256]{2,1,0:T(8,128)(2,1)}) custom-call(bf16[128,64,256]{2,1,0:T(8,128)(2,1)} %get-tuple-element.50.a_ref, bf16[128,64,256]{2,1,0:T(8,128)(2,1)} %get-tuple-element.51.b_ref, bf16[128,256,256]{2,1,0:T(8,128)(2,1)} %get-tuple-element.57.dx_ref), custom_call_target="tpu_custom_call" | custom-call | tf_op jit(solution)/shard_map/grads1/pallas_call | solution.py:679
  249.6 66.2 %midb.1 = (bf16[64,128,256]{2,1,0:T(8,128)(2,1)}, bf16[128,64,256]{2,1,0:T(8,128)(2,1)}, bf16[64,128,256]{2,1,0:T(8,128)(2,1)}, f32[640,128]{1,0:T(8,128)}, f32[...) custom-call(bf16[128,64,256]{2,1,0:T(8,128)(2,1)} %get-tuple-element.58.da_ref, ...), custom_call_target="tpu_custom_call" | custom-call | tf_op jit(solution)/shard_map/midb/pallas_call | solution.py:683
  315.8 19.0 %grads0.1 = (bf16[128,64,256]{2,1,0:T(8,128)(2,1)}, bf16[128,64,256]{2,1,0:T(8,128)(2,1)}) custom-call(bf16[128,64,256]{2,1,0:T(8,128)(2,1)} %get-tuple-element.63.dx_ref, bf16[128,256,256]{2,1,0:T(8,128)(2,1)} %get-tuple-element.46.b_ref, bf16[128,256,128]{2,1,0:T(8,128)(2,1)} %get-tuple-element.64.dxk_ref, bf16[128,256,256]{2,1,0:T(8,128)(2,1)} %get-tuple-element.65.a_ref), custom_call_target="tpu_custom_call" | custom-call | tf_op jit(solution)/shard_map/grads0/pallas_call | solution.py:693
  334.8 37.1 %last.1 = (bf16[64,256,128]{2,1,0:T(8,128)(2,1)}, bf16[64,256,128]{2,1,0:T(8,128)(2,1)}, f32[640,128]{1,0:T(8,128)}, f32[6,128,128]{2,1,0:T(8,128)}) custom-call(bf16[128,64,256]{2,1,0:T(8,128)(2,1)} %get-tuple-element.66.da_ref, bf16[128,64,256]{2,1,0:T(8,128)(2,1)} %get-tuple-element.67.db_ref, bf16[128,128,256]{2,1,0:T(8,128)(2,1)} %get-tuple-element.68.zh_ref, ...), custom_call_target="tpu_custom_call" | custom-call | tf_op jit(solution)/shard_map/last/pallas_call | solution.py:696
  372.0 27.4 %reduce.1 = f32[1664,128]{1,0:T(8,128)} custom-call(f32[640,128]{1,0:T(8,128)} %get-tuple-element.74.dwp0_ref, f32[128,128]{1,0:T(8,128)} %get-tuple-element.75.dwo0_ref, f32[6,128,128]{2,1,0:T(8,128)} %get-tuple-element.76.pre0_ref, f32[4,128,128]{2,1,0:T(8,128)} %get-tuple-element.77.post0_ref, f32[640,128]{1,0:T(8,128)} %get-tuple-element.78.dwp1_ref, ...), custom_call_target="tpu_custom_call" | custom-call | tf_op jit(solution)/shard_map/reduce/pallas_call | solution.py:604
  399.4 1.2 slice.24
  401.7 0.7 slice.37
  402.4 1.1 copy.36
  403.5 0.6 pad_maximum_fusion
  (11 shorter events, 1.4 us)
Async XLA Ops:
  5.7 110.6 %copy-start.1 = (bf16[2,128,128]{2,1,0:T(8,128)(2,1)S(1)}, bf16[2,128,128]{2,1,0:T(8,128)(2,1)}, u32[]{:S(2)}) copy-start(bf16[2,128,128]{2,1,0:T(8,128)(2,1)} %wo_ref.3) | copy-start | bytes 196612
  115.2 81.6 %collective-permute-start = (bf16[48,256,128]{2,1,0:T(8,128)(2,1)}, bf16[48,256,128]{2,1,0:T(8,128)(2,1)S(1)}, u32[]{:S(2)}, u32[]{:S(2)}) collective-permute-start(bf16[48,256,128]{2,1,0:T(8,128)(2,1)} %get-tuple-element.56), channel_id=1, source_target_pairs={{0,2},{2,0},{1,3},{3,1},{4,6},{6,4},{5,7},{7,5},{8,10},{10,8},{9,1... | collective-permute-start | bytes 9437192 | tf_op jit(solution)/shard_map/ppermute | solution.py:657
  196.7 1.7 copy-start

commit v4 on v3

--- a/solution.py
+++ b/solution.py
@@ -61,8 +61,9 @@
 
 
 def by_chip(v):
+    rows = v.shape[0]
     v0, v1 = v[:, :C], v[:, C:]
-    low = lax.broadcasted_iota(jnp.int32, (C, C), 1) < HB
+    low = lax.broadcasted_iota(jnp.int32, (rows, C), 1) < HB
     return jnp.concatenate([jnp.where(low, v0, pltpu.roll(v1, HB, 1)), jnp.where(low, pltpu.roll(v0, HB, 1), v1)], axis=1)
 
 
@@ -192,7 +193,7 @@
     return [pltpu.VMEM((2, C, RB, N), BF16), pltpu.SemaphoreType.DMA((2,)), pltpu.SemaphoreType.DMA((2,)), pltpu.SemaphoreType.DMA((8,))]
 
 
-def pre_kernel(z_ref, dz_ref, m_ref, ln_ref, wt_ref, bp_ref, a_ref, zh_ref, zt_ref, g_ref, mall_ref, af_ref, bf_ref, dzs_ref,
+def pre_kernel(z_ref, dz_ref, m_ref, lni_ref, lnm_ref, bo_ref, bproj_ref, wp_ref, wo_ref, a_ref, zh_ref, zt_ref, g_ref, mall_ref, prm_ref, wt_ref, wot_ref, af_ref, bf_ref, dzs_ref,
                scr_a, scr_b, dzbuf, dzsem, mbuf, zbuf, zloc, zsend, zrecv, msem, st_a, la, sa, ra, st_b, lb, sb, rb_):
     step = pl.program_id(0)
     xb = partner(1)[0]
@@ -225,19 +226,25 @@
     m_dst = mbuf.at[pl.ds(pl.multiple_of(xb * HB, HB), HB), :]
 
     def m_there():
-        return remote(m_ref, m_dst, msem.at[1], msem.at[2], 1)
+        return remote(m_dst, m_dst, msem.at[1], msem.at[2], 1)
 
     @pl.when(step == 0)
     def _():
         for q in range(4):
             z_here(q).start()
+        m_dst[...] = by_chip(m_ref[...].astype(F32))
         greet((0, 1))
-        m_here = pltpu.make_async_copy(m_ref, m_dst, msem.at[0])
-        m_here.start()
         m_there().start()
         for q in range(4):
             z_there(q).start()
-        m_here.wait()
+        for k in range(2):
+            vecs = [ref[k, q:q + 1].astype(F32) for ref in (lni_ref, lnm_ref) for q in range(2)] + [bo_ref[k:k + 1].astype(F32)]
+            vecs += [bproj_ref[k:k + 1, q * C:q * C + C].astype(F32) for q in range(5)]
+            cols = jnp.transpose(jnp.concatenate(vecs + [jnp.zeros((6, C), F32)], axis=0))
+            for q in range(10):
+                prm_ref[k, q] = jnp.broadcast_to(cols[:, q:q + 1], (C, N))
+            wt_ref[k] = jnp.transpose(wp_ref[k])
+            wot_ref[k] = jnp.transpose(wo_ref[k])
     for q in range(4):
         @pl.when(step == q)
         def _():
@@ -253,9 +260,9 @@
         zt = load_t(zbuf, step * RB + r)
         zt_ref[r] = zt.astype(BF16)
         zn, _ = norm(zt)
-        zh = (zn * ln_ref[0] + ln_ref[1]).astype(BF16)
+        zh = (zn * prm_ref[0, 0] + prm_ref[0, 1]).astype(BF16)
         zh_ref[r] = zh
-        gates(zh, mbuf[pl.ds(rb(step) * RB + r, 1), :], wt_ref, bp_ref, scr_a, scr_b, g_ref, r)
+        gates(zh, mbuf[pl.ds(rb(step) * RB + r, 1), :], wt_ref.at[0], prm_ref.at[0, 5:10], scr_a, scr_b, g_ref, r)
         return 0
     lax.fori_loop(0, RB, row, 0, unroll=UN)
     ship(step, [(scr_a, st_a, af_ref, (la, sa, ra), False), (scr_b, st_b, bf_ref, (lb, sb, rb_), False)])
@@ -610,13 +617,6 @@
 
 def solution(mesh):
     def local_step(z_pair, pair_mask, dz_out, ln_in, w_proj, b_proj, ln_mid, w_out, b_out):
-        mask = pair_mask[0].reshape(HB, 2, 2, HB).transpose(0, 2, 1, 3).reshape(HB, N).astype(F32)
-
-        prm = jnp.concatenate([ln_in, ln_mid, b_out[:, None], b_proj.reshape(2, 5, C)], axis=1).astype(F32)
-        prm = jnp.broadcast_to(prm[..., None], (2, 10, C, N))
-        wt = jnp.swapaxes(w_proj, 1, 2)
-        wot = jnp.swapaxes(w_out, 1, 2)
-
         def pick(k, *shape):
             return pl.BlockSpec((None,) + shape, lambda i: (k,) + (0,) * len(shape))
 
@@ -647,12 +647,12 @@
         rt_own = sds((HB, C, N), BF16)
         vm = pl.BlockSpec(memory_space=pltpu.VMEM)
 
-        a0, zh0, zt0, g0, mask_all, a0f, b0f, dz_head = call(
-            pre_kernel, 8, [ANY, ANY, vm] + ln_s(0) + proj_s(0) + bp_s(0),
-            [cm_spec(rb), rows_spec((C, N), rb), rows_spec((C, N), rb), rows_spec((C, N), rb), vm, ANY, ANY, ANY],
-            [cm_all, rt_all, rt_all, rt_f32, sds((C, N), F32), cm_full, cm_full, sds((DZ1, N, C), BF16)],
+        a0, zh0, zt0, g0, mask_all, prm, wt, wot, a0f, b0f, dz_head = call(
+            pre_kernel, 8, [ANY, ANY] + [vm] * 7,
+            [cm_spec(rb), rows_spec((C, N), rb), rows_spec((C, N), rb), rows_spec((C, N), rb), vm, vm, vm, vm, ANY, ANY, ANY],
+            [cm_all, rt_all, rt_all, rt_f32, sds((C, N), F32), sds((2, 10, C, N), F32), sds((2, CP, C), BF16), sds((2, C, C), BF16), cm_full, cm_full, sds((DZ1, N, C), BF16)],
             [scr(), scr(), pltpu.VMEM((DZ1, N, C), BF16), pltpu.SemaphoreType.DMA((2,)), pltpu.VMEM((C, N), F32), pltpu.VMEM((C, N, C), BF16)] + [pltpu.SemaphoreType.DMA((4,))] * 3 + [pltpu.SemaphoreType.DMA((3,))] + ship_scratch() * 2,
-            "pre", 1)(z_pair[0], dz_out[0], mask, prm, wt, prm)
+            "pre", 1)(z_pair[0], dz_out[0], pair_mask[0], ln_in, ln_mid, b_out, b_proj, w_proj, w_out)
         dz_own = dz_out[0]
         dz_oth = lax.ppermute(dz_head, "dap", SWAP_X)
         x0 = jnp.einsum("cik,cjk->cij", a0, b0f, preferred_element_type=F32)

time: 404 us -> 397 us (0.983)
  local copies, waits for them, and re-layouts: 12.6 us -> 5.79 us
  transfers between devices with their start and end apart: 1 -> 1, of which waited for: 0 -> 0; matrix products, arithmetic and copies ran while one was open for 8% -> 8% of each run, Pallas kernels for 12% -> 13%
where the time goes in v4:
time: 397 us; the launch traced here: 396 us
  Pallas kernels  358 us (90%)
  matrix products  29.9 us (8%)
  local copies, waits for them, and re-layouts  5.79 us (1%)
    pallas_call x1, Pallas kernels, local_step(): call(pre_kernel, 8, [ANY, ANY] + [vm] * 7, [cm_spec(rb), rows_spec((C, N)...  108 us
    pallas_call x1, Pallas kernels, local_step(): call(midb_kernel, 4, [cm_spec(same), cm_spec(same), rows_spec((C, N), own...  66.3 us
    pallas_call x1, Pallas kernels, local_step(): call(mid_kernel, 8, [cm_spec(rb), rows_spec((C, N), rb), rows_spec((C, N)...  49.8 us
    pallas_call x1, Pallas kernels, local_step(): call(last_kernel, 4, [cm_spec(same), cm_spec(same), rows_spec((C, N), own...  37.1 us
    pallas_call x1, Pallas kernels, local_step(): call(post1_kernel, 8, [cm_spec(rb), rows_spec((C, N), rb), rows_spec((C,...  34.7 us
    pallas_call x1, Pallas kernels, reduce_all(): pl.pallas_call(reduce_kernel, name='reduce', out_shape=sds((GROWS, C), F3...  27 us
    pallas_call x1, Pallas kernels, local_step(): call(grads0_kernel, C // CB, [chan(HB, N), chan(N, N), chan(N, C), chan(N...  19 us
    pallas_call x1, Pallas kernels, local_step(): call(grads1_kernel, C // CB, [chan(HB, N), chan(HB, N), chan(N, N)], [cha...  16.4 us
  transfers between devices with their start and end apart: 1, of which 0 were waited for; matrix products, arithmetic and copies ran while one was open for 8% of the time, Pallas kernels for 13%

profile of v4, /device:TPU:0, one launch (start us, length us, event | category | flops | bytes accessed | tf_op | source)
XLA Modules:
  0.0 396.3 jit_solution(102355190925971678)
XLA Ops:
  0.6 107.6 %pre.1 = (bf16[128,128,256]{2,1,0:T(8,128)(2,1)}, bf16[128,128,256]{2,1,0:T(8,128)(2,1)}, bf16[128,128,256]{2,1,0:T(8,128)(2,1)}, f32[128,128,256]{2,1,0:T(8,128...) custom-call(bf16[64,256,128]{2,1,0:T(8,128)(2,1)} %bitcast.24, ...), custom_call_target="tpu_custom_call" | custom-call | tf_op jit(solution)/shard_map/pre/pallas_call | solution.py:650
  108.3 1.2 collective-permute-start
  109.4 14.3 %fusion.2.x_ref.x0_ref = f32[128,128,256]{2,1,0:T(8,128)} fusion(bf16[128,128,256]{2,1,0:T(8,128)(2,1)} %get-tuple-element.48, bf16[128,256,256]{2,1,0:T(8,128)(2,1)} %get-tuple-element.49.b_ref), kind=kOutput, calls=%fused_computation.6 | convolution fusion | flops 2147483648 | bytes 41943040 | tf_op jit(solution)/shard_map/cik,cjk->cij/dot_general | solution.py:658
  123.7 49.8 %mid.1 = (bf16[128,128,256]{2,1,0:T(8,128)(2,1)}, bf16[128,128,256]{2,1,0:T(8,128)(2,1)}, f32[128,128,256]{2,1,0:T(8,128)}, bf16[128,64,256]{2,1,0:T(8,128)(2,1)...) custom-call(f32[128,128,256]{2,1,0:T(8,128)} %fusion.2.x_ref.x0_ref, ...), custom_call_target="tpu_custom_call" | custom-call | tf_op jit(solution)/shard_map/mid/pallas_call | solution.py:660
  173.6 15.6 %fusion.3.x_ref = f32[128,128,256]{2,1,0:T(8,128)} fusion(bf16[128,256,128]{2,1,0:T(8,128)(2,1)} %get-tuple-element.58, bf16[128,256,256]{2,1,0:T(8,128)(2,1)} %get-tuple-element.59), kind=kOutput, calls=%fused_computation.7 | convolution fusion | flops 2147483648 | bytes 41943040 | tf_op jit(solution)/shard_map/cki,ckj->cij/dot_general | solution.py:667
  189.2 0.0 collective-permute-done.dzo_ref
  189.2 0.0 copy-start
  189.2 1.7 copy-done
  190.9 34.7 %post1.1 = (bf16[64,128,256]{2,1,0:T(8,128)(2,1)}, bf16[64,128,256]{2,1,0:T(8,128)(2,1)}, bf16[64,128,256]{2,1,0:T(8,128)(2,1)}, f32[128,128]{1,0:T(8,128)}, f32...) custom-call(f32[128,128,256]{2,1,0:T(8,128)} %fusion.3.x_ref, f32[128,128,256]{2,1,0:T(8,128)} %get-tuple-element.60.g_ref, ...), custom_call_target="tpu_custom_call" | custom-call | tf_op jit(solution)/shard_map/post1/pallas_call | solution.py:671
  225.6 16.4 %grads1.1 = (bf16[128,64,256]{2,1,0:T(8,128)(2,1)}, bf16[128,64,256]{2,1,0:T(8,128)(2,1)}) custom-call(bf16[128,64,256]{2,1,0:T(8,128)(2,1)} %get-tuple-element.56.a_ref, bf16[128,64,256]{2,1,0:T(8,128)(2,1)} %get-tuple-element.57.b_ref, bf16[128,256,256]{2,1,0:T(8,128)(2,1)} %get-tuple-element.63.dx_ref), custom_call_target="tpu_custom_call" | custom-call | tf_op jit(solution)/shard_map/grads1/pallas_call | solution.py:679
  242.1 66.3 %midb.1 = (bf16[64,128,256]{2,1,0:T(8,128)(2,1)}, bf16[128,64,256]{2,1,0:T(8,128)(2,1)}, bf16[64,128,256]{2,1,0:T(8,128)(2,1)}, f32[640,128]{1,0:T(8,128)}, f32[...) custom-call(bf16[128,64,256]{2,1,0:T(8,128)(2,1)} %get-tuple-element.64.da_ref, ...), custom_call_target="tpu_custom_call" | custom-call | tf_op jit(solution)/shard_map/midb/pallas_call | solution.py:683
  308.4 19.0 %grads0.1 = (bf16[128,64,256]{2,1,0:T(8,128)(2,1)}, bf16[128,64,256]{2,1,0:T(8,128)(2,1)}) custom-call(bf16[128,64,256]{2,1,0:T(8,128)(2,1)} %get-tuple-element.69.dx_ref, bf16[128,256,256]{2,1,0:T(8,128)(2,1)} %get-tuple-element.49.b_ref, bf16[128,256,128]{2,1,0:T(8,128)(2,1)} %get-tuple-element.70.dxk_ref, bf16[128,256,256]{2,1,0:T(8,128)(2,1)} %get-tuple-element.71.a_ref), custom_call_target="tpu_custom_call" | custom-call | tf_op jit(solution)/shard_map/grads0/pallas_call | solution.py:693
  327.4 37.1 %last.1 = (bf16[64,256,128]{2,1,0:T(8,128)(2,1)}, bf16[64,256,128]{2,1,0:T(8,128)(2,1)}, f32[640,128]{1,0:T(8,128)}, f32[6,128,128]{2,1,0:T(8,128)}) custom-call(bf16[128,64,256]{2,1,0:T(8,128)(2,1)} %get-tuple-element.72.da_ref, bf16[128,64,256]{2,1,0:T(8,128)(2,1)} %get-tuple-element.73.db_ref, bf16[128,128,256]{2,1,0:T(8,128)(2,1)} %get-tuple-element.74.zh_ref, ...), custom_call_target="tpu_custom_call" | custom-call | tf_op jit(solution)/shard_map/last/pallas_call | solution.py:696
  364.5 27.0 %reduce.1 = f32[1664,128]{1,0:T(8,128)} custom-call(f32[640,128]{1,0:T(8,128)} %get-tuple-element.80.dwp0_ref, f32[128,128]{1,0:T(8,128)} %get-tuple-element.81.dwo0_ref, f32[6,128,128]{2,1,0:T(8,128)} %get-tuple-element.82.pre0_ref, f32[4,128,128]{2,1,0:T(8,128)} %get-tuple-element.83.post0_ref, f32[640,128]{1,0:T(8,128)} %get-tuple-element.84.dwp1_ref, ...), custom_call_target="tpu_custom_call" | custom-call | tf_op jit(solution)/shard_map/reduce/pallas_call | solution.py:611
  391.6 1.2 slice.24
  392.8 0.6 fusion
  393.3 0.6 fusion.1
  393.9 0.7 slice.37
  394.6 1.1 copy.19
  395.7 0.6 pad_maximum_fusion
  (3 shorter events, 0.0 us)
Async XLA Ops:
  108.3 81.0 %collective-permute-start = (bf16[48,256,128]{2,1,0:T(8,128)(2,1)}, bf16[48,256,128]{2,1,0:T(8,128)(2,1)S(1)}, u32[]{:S(2)}, u32[]{:S(2)}) collective-permute-start(bf16[48,256,128]{2,1,0:T(8,128)(2,1)} %get-tuple-element.62), channel_id=1, source_target_pairs={{0,2},{2,0},{1,3},{3,1},{4,6},{6,4},{5,7},{7,5},{8,10},{10,8},{9,1... | collective-permute-start | bytes 9437192 | tf_op jit(solution)/shard_map/ppermute | solution.py:657
  189.2 1.7 copy-start
